TPU v7x, 32 devices: a whole 2x2x4 slice. The times are simulated.
32 devices in a mesh: seq: 8 (over y, x, core), chan: 4 (over z).
Axes of the slice: x: 2, y: 2, z: 4, core: 2. Of those that a mesh axis runs over, the one named last changes fastest.
Arguments:
- fwd_q: bfloat16 [1024, 4096], P('seq', 'chan'), may hold values from -6 to 6
- fwd_k: bfloat16 [1024, 4096], P('seq', 'chan'), may hold values from -6 to 6
- fwd_v: bfloat16 [1024, 4096], P('seq', 'chan'), may hold values from -6 to 6
- bwd_q: bfloat16 [1024, 4096], P('seq', 'chan'), may hold values from -6 to 6
- bwd_k: bfloat16 [1024, 4096], P('seq', 'chan'), may hold values from -6 to 6
- bwd_v: bfloat16 [1024, 4096], P('seq', 'chan'), may hold values from -6 to 6
- bwd_grad: bfloat16 [1024, 4096], P('seq', 'chan'), may hold values from -6 to 6
- filters: float32 [1024, 1024], P('seq', 'chan'), may hold values from -0.1875 to 0.1875
- skip: float32 [4096], P('chan'), may hold values from -4 to 4
Outputs:
- output: bfloat16 [1024, 4096], P('seq', 'chan')
- grad_query: bfloat16 [1024, 4096], P('seq', 'chan')
- grad_key: bfloat16 [1024, 4096], P('seq', 'chan')
- grad_value: bfloat16 [1024, 4096], P('seq', 'chan')
- grad_filter: float32 [1024, 1024], P('seq', 'chan')
- grad_skip: float32 [4096], P('chan')
All inputs are finite; a program needn't handle non-finite values.
Results may differ from a plain program's by a relative error of at most 0.0075.
Values may be sent and summed in bfloat16 or wider, within the bound.
A program may use at most 256 MiB of HBM per device.

v0:
```python
import functools
import math

import jax
import jax.numpy as jnp
import numpy as np
from jax import lax
from jax.experimental import pallas as pl
from jax.experimental.pallas import tpu as pltpu
from jax.sharding import PartitionSpec as P

HIGHEST = lax.Precision.HIGHEST
LANES = 128
MESH = pl.DeviceIdType.MESH
BF16 = jnp.bfloat16
F32 = jnp.float32


def index_ramp(total):
    return jnp.arange(total, dtype=jnp.int32)


def widened(values):
    return values.astype(jnp.float32)


def angles(out_index, in_index, period, sign):
    phase_steps = out_index[:, None] * in_index[None, :] % period
    phase = phase_steps.astype(jnp.float32) * (sign * 2.0 * math.pi / period)
    return (jnp.cos(phase), jnp.sin(phase))


def times_table(left, right):
    return (left[0] * right[0] - left[1] * right[1], left[0] * right[1] + left[1] * right[0])


def block_table(pair):
    cosine, sine_part = pair
    return jnp.stack([jnp.stack([cosine, -sine_part]), jnp.stack([sine_part, cosine])])


def product_of(left, right):
    return jnp.stack(
        [left[0] * right[0] - left[1] * right[1], left[0] * right[1] + left[1] * right[0]]
    )


def conj_product(left, right):
    return jnp.stack(
        [left[0] * right[0] + left[1] * right[1], left[0] * right[1] - left[1] * right[0]]
    )


def joined(left, right):
    return jnp.concatenate([left, right], axis=-1)


def factor(total):
    chosen = 1
    for candidate in range(1, total + 1):
        if candidate * candidate <= total and total % candidate == 0:
            chosen = candidate
    return chosen


def leading_section(values, seq_size):
    cosine, sine_part = angles(index_ramp(2 * seq_size), index_ramp(seq_size), 2 * seq_size, -1.0)
    table = jnp.stack([cosine, sine_part])
    return jnp.einsum("rkp,pmc->rkmc", table, values, precision=HIGHEST)


def trailing_section(values, seq_size, period):
    cosine, sine_part = angles(index_ramp(seq_size), index_ramp(2 * seq_size), 2 * seq_size, 1.0)
    table = jnp.stack([cosine, -sine_part]) * (1.0 / period)
    return jnp.einsum("rpk,rkmc->pmc", table, values, precision=HIGHEST)


def inner_forward(values, freq_keys, period):
    lead_size, row_count, chan_count = values.shape[1:]
    outer_size = factor(row_count)
    inner_size = row_count // outer_size
    values = values.reshape(2, lead_size, outer_size, inner_size, chan_count)
    first_twiddle = angles(freq_keys, index_ramp(row_count), period, -1.0)
    first_twiddle = tuple(
        (part.reshape(lead_size, outer_size, inner_size) for part in first_twiddle)
    )
    outer_dft = angles(index_ramp(outer_size), index_ramp(outer_size), outer_size, -1.0)
    outer_table = times_table(
        tuple((part[None, :, :, None] for part in outer_dft)),
        tuple((part[:, None, :, :] for part in first_twiddle)),
    )
    values = jnp.einsum("rsjxab,sjabc->rjxbc", block_table(outer_table), values, precision=HIGHEST)
    second_twiddle = angles(index_ramp(outer_size), index_ramp(inner_size), row_count, -1.0)
    inner_dft = angles(index_ramp(inner_size), index_ramp(inner_size), inner_size, -1.0)
    inner_table = times_table(
        tuple((part[None, :, :] for part in inner_dft)),
        tuple((part[:, None, :] for part in second_twiddle)),
    )
    return jnp.einsum("rsxyb,sjxbc->rjxyc", block_table(inner_table), values, precision=HIGHEST)


def inner_inverse(values, freq_keys, period):
    lead_size, outer_size, inner_size, chan_count = values.shape[1:]
    row_count = outer_size * inner_size
    second_twiddle = angles(index_ramp(outer_size), index_ramp(inner_size), row_count, 1.0)
    inner_dft = angles(index_ramp(inner_size), index_ramp(inner_size), inner_size, 1.0)
    inner_table = times_table(
        tuple((part[:, :, None] for part in second_twiddle)),
        tuple((part[None, :, :] for part in inner_dft)),
    )
    values = jnp.einsum("rsxby,sjxyc->rjxbc", block_table(inner_table), values, precision=HIGHEST)
    first_twiddle = angles(freq_keys, index_ramp(row_count), period, 1.0)
    first_twiddle = tuple(
        (part.reshape(lead_size, outer_size, inner_size) for part in first_twiddle)
    )
    outer_dft = angles(index_ramp(outer_size), index_ramp(outer_size), outer_size, 1.0)
    outer_table = times_table(
        tuple((part[:, :, :, None] for part in first_twiddle)),
        tuple((part[None, :, None, :] for part in outer_dft)),
    )
    values = jnp.einsum("rsjabx,sjxbc->rjabc", block_table(outer_table), values, precision=HIGHEST)
    return values.reshape(2, lead_size, row_count, chan_count)


def forward_local(signal_part, seq_size):
    seq_length, chan_count = signal_part.shape
    row_count = seq_length // seq_size
    values = leading_section(signal_part.reshape(seq_size, row_count, chan_count), seq_size)
    return inner_forward(values, index_ramp(2 * seq_size), 2 * seq_length)


def inverse_local(values, seq_size):
    lead_size, outer_size, inner_size, chan_count = values.shape[1:]
    row_count = outer_size * inner_size
    period = 2 * seq_size * row_count
    values = inner_inverse(values, index_ramp(2 * seq_size), period)
    return trailing_section(values, seq_size, period).reshape(seq_size * row_count, chan_count)


def filter_times_pair(spec_filter, spec_pair):
    shape_pair = spec_pair.shape
    width = spec_filter.shape[-1]
    pair_view = spec_pair.reshape(shape_pair[:-1] + (2, width))
    filter_view = spec_filter[..., None, :]
    return product_of(filter_view, pair_view).reshape(shape_pair)


def per_device(fwd_q, fwd_k, fwd_v, bwd_q, bwd_k, bwd_v, bwd_grad, filters, skip):
    row_count, chan_width = fwd_q.shape
    seq_size = lax.axis_size("seq")
    grad_scale = 1.0 / math.sqrt(row_count * seq_size)
    source = (widened(fwd_k) * widened(fwd_v)).astype(jnp.bfloat16)
    second_source = (widened(bwd_k) * widened(bwd_v)).astype(jnp.bfloat16)
    upstream = (widened(bwd_grad) * widened(bwd_q)).astype(jnp.bfloat16)
    skip_gain = widened(skip)
    filters_all = lax.all_gather(filters, "chan", axis=1, tiled=True)
    narrow = chan_width // seq_size
    local_first, local_second = (
        lax.all_to_all(source, "seq", split_axis=1, concat_axis=0, tiled=True),
        lax.all_to_all(second_source, "seq", split_axis=1, concat_axis=0, tiled=True),
    )
    local_filter = lax.all_to_all(filters_all, "seq", split_axis=1, concat_axis=0, tiled=True)
    local_up = lax.all_to_all(upstream, "seq", split_axis=1, concat_axis=0, tiled=True)
    spec_sources = forward_local(
        widened(jnp.concatenate([local_first, local_second], axis=1)), seq_size
    )
    spec_filter = forward_local(local_filter, seq_size)
    conv_local = inverse_local(filter_times_pair(spec_filter, spec_sources), seq_size)
    conv_first, conv_second = (
        lax.all_to_all(conv_local[:, :narrow], "seq", split_axis=0, concat_axis=1, tiled=True),
        lax.all_to_all(conv_local[:, narrow:], "seq", split_axis=0, concat_axis=1, tiled=True),
    )
    spec_up = forward_local(widened(local_up), seq_size)
    spec_second = spec_sources[..., narrow:]
    back_local = inverse_local(
        joined(conj_product(spec_filter, spec_up), conj_product(spec_second, spec_up)), seq_size
    )
    through_conv, filter_terms = (
        lax.all_to_all(back_local[:, :narrow], "seq", split_axis=0, concat_axis=1, tiled=True),
        lax.all_to_all(
            back_local[:, narrow:] * grad_scale, "seq", split_axis=0, concat_axis=1, tiled=True
        ),
    )
    grad_filter = lax.psum_scatter(filter_terms, "chan", scatter_dimension=1, tiled=True)
    source_wide = widened(source)
    second_wide = widened(second_source)
    upstream_wide = widened(upstream)
    mixed = conv_first + skip_gain * source_wide
    output = (widened(fwd_q) * mixed).astype(jnp.bfloat16)
    mixed_two = conv_second + skip_gain * second_wide
    grad_query = (widened(bwd_grad) * mixed_two).astype(jnp.bfloat16)
    through = through_conv + skip_gain * upstream_wide
    grad_key = (through * widened(bwd_v)).astype(jnp.bfloat16)
    grad_value = (through * widened(bwd_k)).astype(jnp.bfloat16)
    grad_skip = lax.psum(jnp.sum(upstream_wide * second_wide, axis=0) * grad_scale, "seq")
    return (output, grad_query, grad_key, grad_value, grad_filter, grad_skip)


def block_tables(rows):
    freq = 2 * np.arange(rows)[:, None] + 1
    phase = (freq * np.arange(rows)[None, :] % (4 * rows)) * (np.pi / (2 * rows))
    forward = np.concatenate([np.cos(phase), -np.sin(phase)], axis=0)
    inverse = np.concatenate([np.cos(phase), -np.sin(phase)], axis=0).T / rows
    return forward.astype(np.float32), inverse.astype(np.float32)


def kernel(
    n, nc, scale,
    fq_h, fk_h, fv_h, bq_h, bk_h, bv_h, bg_h, filt_h, skip_h, fwd_h, inv_h,
    out_h, gq_h, gk_h, gv_h, gf_h, gs_h,
    fq, fk, fv, bq, bk, bv, bg, filt, skip, fwd_t, inv_t, in_sem,
    out_o, gq_o, gk_o, gv_o, gf_o, gs_o, out_sem,
    su_send, s1_send, fz, su, s1, rf, spec_s, spec_u, spec_f, spec_w, prod,
    c_send, c_recv, g_send, rg, zg, k_send, k_recv,
    su_ss, su_rs, s1_ss, s1_rs, f_ss, f_rs, z_ss, z_rs, c_ss, c_rs, g_ss, g_rs, y_ss, y_rs, k_ss, k_rs,
):
    rows, chan_width = fq.shape
    w = chan_width // n
    per = filt.shape[1] // w
    me = lax.axis_index("seq")
    mz = lax.axis_index("chan")
    peers = [lax.rem(me + r, n) for r in range(1, n)]
    senders = peers[::-1]
    zpeers = [lax.rem(mz + r, nc) for r in range(1, nc)]
    started = []

    def lane(p):
        return pl.ds(pl.multiple_of(p * w, w), w)

    def copy(src, dst, ss, rs, to):
        return pltpu.make_async_remote_copy(
            src_ref=src, dst_ref=dst, send_sem=ss, recv_sem=rs, device_id=to, device_id_type=MESH
        )

    def send(src, dst, ss, rs, to):
        c = copy(src, dst, ss, rs, to)
        c.start()
        started.append(c)

    def arrived(buf, ss, rs, to):
        copy(buf, buf, ss, rs, to).wait_recv()

    loads = {}
    order = ((filt_h, filt), (bk_h, bk), (bv_h, bv), (bg_h, bg), (bq_h, bq), (fk_h, fk), (fv_h, fv))
    for at, (far, near) in enumerate(order + ((fwd_h, fwd_t), (inv_h, inv_t), (skip_h, skip), (fq_h, fq))):
        loads[id(near)] = pltpu.make_async_copy(far, near, in_sem.at[at])
        loads[id(near)].start()

    def loaded(*refs):
        for ref in refs:
            loads[id(ref)].wait()

    stores = []

    def store(near, far):
        c = pltpu.make_async_copy(near, far, out_sem.at[len(stores)])
        c.start()
        stores.append(c)

    barrier = pltpu.get_barrier_semaphore()
    for p in peers:
        pl.semaphore_signal(barrier, inc=1, device_id={"seq": p}, device_id_type=MESH)
    for z in zpeers:
        pl.semaphore_signal(barrier, inc=1, device_id={"chan": z}, device_id_type=MESH)

    def transform(dst, q, block):
        dst[q] = jnp.dot(fwd_t[...], block, preferred_element_type=F32)

    def gate_block(p):
        at = lane(p)
        su_send[p, 0] = (bk[:, at].astype(F32) * bv[:, at].astype(F32)).astype(BF16)
        su_send[p, 1] = (bg[:, at].astype(F32) * bq[:, at].astype(F32)).astype(BF16)

    loaded(filt)
    for h in range(per):
        fz[mz * per + h] = filt[:, h * w:(h + 1) * w].astype(BF16)
    pl.semaphore_wait(barrier, n - 1 + nc - 1)
    for z in zpeers:
        part = fz.at[pl.ds(mz * per, per)]
        send(part, part, z_ss.at[z], z_rs.at[mz], {"chan": z})
    loaded(bk, bv, bg, bq)
    for p in peers:
        gate_block(p)
        send(su_send.at[p], su.at[me], su_ss.at[p], su_rs.at[me], {"seq": p})
    gate_block(me)
    su[me] = su_send[me]
    loaded(fk, fv)
    for p in range(n):
        cols = slice(p * w, (p + 1) * w)
        s1_send[p] = (fk[:, cols].astype(F32) * fv[:, cols].astype(F32)).astype(BF16)
    s1[me] = s1_send[me]
    loaded(fwd_t, inv_t)
    transform(spec_s, me, su[me, 0])
    transform(spec_u, me, su[me, 1])
    for z in zpeers:
        arrived(fz.at[pl.ds(z * per, per)], z_ss.at[z], z_rs.at[z], {"chan": z})
    for p in peers:
        send(fz.at[p], rf.at[me], f_ss.at[p], f_rs.at[me], {"seq": p})
    for p in peers:
        send(s1_send.at[p], s1.at[me], s1_ss.at[p], s1_rs.at[me], {"seq": p})
    rf[me] = fz[me]

    sign = 1.0 - 2.0 * lax.rem(lax.broadcasted_iota(jnp.int32, (rows, w), 0), 2).astype(F32)

    def windowed(src):
        spec_w[0] = src[0]
        for d in range(1, n):
            spec_w[d, :rows] = src[d, :rows] - sign * src[d - 1, rows:]
            spec_w[d, rows:] = src[d, rows:] + sign * src[d - 1, :rows]

    def products(src, corr):
        def tile(k, carry):
            re_at = pl.ds(pl.multiple_of(k * 8, 8), 8)
            im_at = pl.ds(pl.multiple_of(rows + k * 8, 8), 8)
            ar = [spec_w[d, re_at] for d in range(n)]
            ai = [spec_w[d, im_at] for d in range(n)]
            xr = [src[d, re_at] for d in range(n)]
            xi = [src[d, im_at] for d in range(n)]
            for b in range(n):
                terms = [(c - b, c) for c in range(b, n)] if corr else [(b - c, c) for c in range(b + 1)]
                re, im = None, None
                for d, c in terms:
                    if corr:
                        tr = ar[d] * xr[c] + ai[d] * xi[c]
                        ti = ar[d] * xi[c] - ai[d] * xr[c]
                    else:
                        tr = ar[d] * xr[c] - ai[d] * xi[c]
                        ti = ar[d] * xi[c] + ai[d] * xr[c]
                    re = tr if re is None else re + tr
                    im = ti if im is None else im + ti
                prod[b, re_at] = re
                prod[b, im_at] = im
            return carry

        lax.fori_loop(0, rows // 8, tile, 0)

    def inverse(b):
        return jnp.dot(inv_t[...], prod[b].astype(BF16), preferred_element_type=F32)

    def give_back(which):
        for p in peers:
            c_send[which, p] = inverse(p).astype(BF16)
            send(c_send.at[which, p], c_recv.at[which, me], c_ss.at[which, p], c_rs.at[which, me], {"seq": p})
        c_recv[which, me] = inverse(me).astype(BF16)

    total = jnp.zeros((1, w), F32)
    for q in [me] + senders:
        if q is not me:
            arrived(su.at[q], su_ss.at[q], su_rs.at[q], {"seq": q})
            transform(spec_s, q, su[q, 0])
            transform(spec_u, q, su[q, 1])
        total += jnp.sum(su[q, 0].astype(F32) * su[q, 1].astype(F32), axis=0, keepdims=True)
    k_send[...] = jnp.broadcast_to(total * scale, k_send.shape)
    for p in peers:
        send(k_send, k_recv.at[me], k_ss.at[p], k_rs.at[me], {"seq": p})
    k_recv[me] = k_send[...]

    windowed(spec_s)
    products(spec_u, True)
    for p in peers:
        g_send[p] = (inverse(p) * scale).astype(BF16)
        send(g_send.at[p], rg.at[me], g_ss.at[p], g_rs.at[me], {"seq": p})
    rg[me] = (inverse(me) * scale).astype(BF16)

    for q in [me] + senders:
        if q is not me:
            arrived(rf.at[q], f_ss.at[q], f_rs.at[q], {"seq": q})
        transform(spec_f, q, rf[q])
    windowed(spec_f)
    products(spec_s, False)
    give_back(0)
    products(spec_u, True)
    give_back(1)

    for q in [me] + senders:
        if q is not me:
            arrived(s1.at[q], s1_ss.at[q], s1_rs.at[q], {"seq": q})
        transform(spec_s, q, s1[q])
    products(spec_s, False)
    give_back(2)

    for q in senders:
        arrived(rg.at[q], g_ss.at[q], g_rs.at[q], {"seq": q})
    for z in zpeers:
        send(rg.at[pl.ds(z * per, per)], zg.at[mz], y_ss.at[z], y_rs.at[mz], {"chan": z})

    loaded(skip, fq)
    for q in [me] + senders:
        at = lane(q)
        gain = skip[:, at]
        if q is not me:
            arrived(c_recv.at[0, q], c_ss.at[0, q], c_rs.at[0, q], {"seq": q})
        mixed = c_recv[0, q].astype(F32) + gain * su_send[q, 0].astype(F32)
        gq_o[:, at] = (bg[:, at].astype(F32) * mixed).astype(BF16)
    store(gq_o, gq_h)
    for q in [me] + senders:
        at = lane(q)
        gain = skip[:, at]
        if q is not me:
            arrived(c_recv.at[1, q], c_ss.at[1, q], c_rs.at[1, q], {"seq": q})
        through = c_recv[1, q].astype(F32) + gain * su_send[q, 1].astype(F32)
        gk_o[:, at] = (through * bv[:, at].astype(F32)).astype(BF16)
        gv_o[:, at] = (through * bk[:, at].astype(F32)).astype(BF16)
    store(gk_o, gk_h)
    store(gv_o, gv_h)
    for z in zpeers:
        arrived(zg.at[z], y_ss.at[z], y_rs.at[z], {"chan": z})
    for h in range(per):
        acc = rg[mz * per + h].astype(F32)
        for z in zpeers:
            acc += zg[z, h].astype(F32)
        gf_o[:, h * w:(h + 1) * w] = acc
    store(gf_o, gf_h)
    for q in senders:
        arrived(k_recv.at[q], k_ss.at[q], k_rs.at[q], {"seq": q})
    for q in range(n):
        gs_o[:, q * w:(q + 1) * w] = k_recv[q, 0:1]
    store(gs_o, gs_h)
    for q in [me] + senders:
        at = lane(q)
        gain = skip[:, at]
        if q is not me:
            arrived(c_recv.at[2, q], c_ss.at[2, q], c_rs.at[2, q], {"seq": q})
        mixed = c_recv[2, q].astype(F32) + gain * s1_send[q].astype(F32)
        out_o[:, at] = (fq[:, at].astype(F32) * mixed).astype(BF16)
    store(out_o, out_h)
    for c in started:
        c.wait_send()
    for c in stores:
        c.wait()


def store_all(*refs):
    count = len(refs) // 3
    far, out, near = refs[:count], refs[count:2 * count], refs[2 * count:-1]
    sems = refs[-1]
    loads = [pltpu.make_async_copy(far[i], near[i], sems.at[0, i]) for i in range(count)]
    stores = [pltpu.make_async_copy(near[i], out[i], sems.at[1, i]) for i in range(count)]
    for c in loads:
        c.start()
    for i in range(count):
        loads[i].wait()
        stores[i].start()
    for c in stores:
        c.wait()


def fused_device(n, nc, *args):
    fwd_q, filters, skip = args[0], args[7], args[8]
    rows, chan_width = fwd_q.shape
    w = chan_width // n
    per = filters.shape[1] // w
    scale = 1.0 / math.sqrt(rows * n)
    forward, inverse = (jnp.asarray(t, dtype=BF16) for t in block_tables(rows))
    wide = jax.ShapeDtypeStruct((rows, chan_width), BF16)
    results = [
        *[pltpu.VMEM((rows, chan_width), BF16)] * 4, pltpu.VMEM(filters.shape, F32), pltpu.VMEM((1, chan_width), F32),
    ]
    dma = pltpu.SemaphoreType.DMA
    block = (n, rows, w)
    spectrum = (n, 2 * rows, w)
    scratch = [
        *[pltpu.VMEM((rows, chan_width), BF16)] * 7, pltpu.VMEM(filters.shape, F32),
        pltpu.VMEM((1, chan_width), F32), pltpu.VMEM(forward.shape, BF16), pltpu.VMEM(inverse.shape, BF16),
        dma((11,)),
        *results, dma((6,)),
        pltpu.VMEM((n, 2, rows, w), BF16), pltpu.VMEM(block, BF16), pltpu.VMEM(block, BF16),
        pltpu.VMEM((n, 2, rows, w), BF16), pltpu.VMEM(block, BF16), pltpu.VMEM(block, BF16),
        *[pltpu.VMEM(spectrum, F32)] * 5,
        pltpu.VMEM((3,) + block, BF16), pltpu.VMEM((3,) + block, BF16),
        pltpu.VMEM(block, BF16), pltpu.VMEM(block, BF16), pltpu.VMEM((nc, per, rows, w), BF16),
        pltpu.VMEM((8, w), F32), pltpu.VMEM((n, 8, w), F32),
        dma((n,)), dma((n,)), dma((n,)), dma((n,)), dma((n,)), dma((n,)), dma((nc,)), dma((nc,)),
        dma((3, n)), dma((3, n)), dma((n,)), dma((n,)), dma((nc,)), dma((nc,)), dma((n,)), dma((n,)),
    ]
    full = 67_000_000
    hbm = pl.BlockSpec(memory_space=pltpu.HBM)
    outs = pl.pallas_call(
        functools.partial(kernel, n, nc, scale),
        out_shape=(
            wide, wide, wide, wide,
            jax.ShapeDtypeStruct(filters.shape, F32), jax.ShapeDtypeStruct((1, chan_width), F32),
        ),
        in_specs=[hbm] * 11,
        out_specs=(hbm,) * 6,
        scratch_shapes=scratch,
        compiler_params=pltpu.CompilerParams(
            collective_id=0, has_side_effects=True, vmem_limit_bytes=full
        ),
    )(*args[:8], skip.reshape(1, chan_width), forward, inverse)
    outs = pl.pallas_call(
        store_all,
        out_shape=tuple(jax.ShapeDtypeStruct(o.shape, o.dtype) for o in outs),
        in_specs=[hbm] * 6,
        out_specs=(hbm,) * 6,
        scratch_shapes=[*results, dma((2, 6))],
        compiler_params=pltpu.CompilerParams(vmem_limit_bytes=full),
    )(*outs)
    return tuple(outs[:5]) + (outs[5].reshape(chan_width),)


def routed(*args):
    n, nc = lax.axis_size("seq"), lax.axis_size("chan")
    rows, chan_width = args[0].shape
    filter_width = args[7].shape[1]
    fits = chan_width % (n * LANES) == 0 and rows % 16 == 0
    if fits and filter_width * nc == chan_width and filter_width % (chan_width // n) == 0:
        return fused_device(n, nc, *args)
    return per_device(*args)


def solution(mesh):
    return jax.shard_map(
        routed,
        mesh=mesh,
        in_specs=(
            P("seq", "chan"),
            P("seq", "chan"),
            P("seq", "chan"),
            P("seq", "chan"),
            P("seq", "chan"),
            P("seq", "chan"),
            P("seq", "chan"),
            P("seq", "chan"),
            P("chan"),
        ),
        out_specs=(
            P("seq", "chan"),
            P("seq", "chan"),
            P("seq", "chan"),
            P("seq", "chan"),
            P("seq", "chan"),
            P("chan"),
        ),
        check_vma=False,
    )
```

profile of v0, /device:TPU:0, one launch (start us, length us, event | category | flops | bytes accessed | tf_op | source)
XLA Modules:
  0.0 36.7 jit_solution(7205605513673105369)
XLA Ops:
  0.6 34.0 %shard_map.154 = (bf16[128,1024]{1,0:T(8,128)(2,1)}, bf16[128,1024]{1,0:T(8,128)(2,1)}, bf16[128,1024]{1,0:T(8,128)(2,1)}, bf16[128,1024]{1,0:T(8,128)(2,1)}, f32[128,256]{1,0:T(8,128)}, /*index=5*/f32[1,1024]{1,0:T(1,128)}) custom-call(bf16[128,1024]{1,0:T(8,128)(2,1)} %fq_h.1, bf16[128,1024]{1,0:T(8,128)(2,1)} %fk_h.1, bf16[128,1024]{1,0:T(8,128)(2,1)} %fv_h.1, ...), custom_call_target="tpu_custom_call" | custom-call | tf_op jit(solution)/shard_map/pallas_call | solution.py:478
  34.7 2.1 %shard_map.155 = (bf16[128,1024]{1,0:T(8,128)(2,1)}, bf16[128,1024]{1,0:T(8,128)(2,1)}, bf16[128,1024]{1,0:T(8,128)(2,1)}, bf16[128,1024]{1,0:T(8,128)(2,1)}, f32[128,256]{1,0:T(8,128)}, /*index=5*/f32[1,1024]{1,0:T(1,128)}) custom-call(bf16[128,1024]{1,0:T(8,128)(2,1)} %get-tuple-element.18.refs_0_, bf16[128,1024]{1,0:T(8,128)(2,1)} %get-tuple-element.19.refs_1_, ...), custom_call_target="tpu_custom_call" | custom-call | tf_op jit(solution)/shard_map/pallas_call | solution.py:491
where the time goes:
time: 36.9 us; the launch traced here: 36.7 us
  Pallas kernels  36.1 us (98%)
  between operations  0.64 us (2%)
    pallas_call x1, Pallas kernels, fused_device(): pl.pallas_call(functools.partial(kernel, n, nc, scale), out_shape=(wide,...  34 us
    pallas_call x1, Pallas kernels, fused_device(): pl.pallas_call(store_all, out_shape=tuple((jax.ShapeDtypeStruct(o.shape,...  2.06 us

commit v1 on v0

--- a/solution.py
+++ b/solution.py
@@ -14,6 +14,7 @@
 MESH = pl.DeviceIdType.MESH
 BF16 = jnp.bfloat16
 F32 = jnp.float32
+KERNEL_VMEM = 32 * 2**20
 
 
 def index_ramp(total):
@@ -207,9 +208,8 @@
 def kernel(
     n, nc, scale,
     fq_h, fk_h, fv_h, bq_h, bk_h, bv_h, bg_h, filt_h, skip_h, fwd_h, inv_h,
-    out_h, gq_h, gk_h, gv_h, gf_h, gs_h,
+    out_o, gq_o, gk_o, gv_o, gf_o, gs_o,
     fq, fk, fv, bq, bk, bv, bg, filt, skip, fwd_t, inv_t, in_sem,
-    out_o, gq_o, gk_o, gv_o, gf_o, gs_o, out_sem,
     su_send, s1_send, fz, su, s1, rf, spec_s, spec_u, spec_f, spec_w, prod,
     c_send, c_recv, g_send, rg, zg, k_send, k_recv,
     su_ss, su_rs, s1_ss, s1_rs, f_ss, f_rs, z_ss, z_rs, c_ss, c_rs, g_ss, g_rs, y_ss, y_rs, k_ss, k_rs,
@@ -249,13 +249,6 @@
     def loaded(*refs):
         for ref in refs:
             loads[id(ref)].wait()
-
-    stores = []
-
-    def store(near, far):
-        c = pltpu.make_async_copy(near, far, out_sem.at[len(stores)])
-        c.start()
-        stores.append(c)
 
     barrier = pltpu.get_barrier_semaphore()
     for p in peers:
@@ -392,7 +385,6 @@
             arrived(c_recv.at[0, q], c_ss.at[0, q], c_rs.at[0, q], {"seq": q})
         mixed = c_recv[0, q].astype(F32) + gain * su_send[q, 0].astype(F32)
         gq_o[:, at] = (bg[:, at].astype(F32) * mixed).astype(BF16)
-    store(gq_o, gq_h)
     for q in [me] + senders:
         at = lane(q)
         gain = skip[:, at]
@@ -401,8 +393,6 @@
         through = c_recv[1, q].astype(F32) + gain * su_send[q, 1].astype(F32)
         gk_o[:, at] = (through * bv[:, at].astype(F32)).astype(BF16)
         gv_o[:, at] = (through * bk[:, at].astype(F32)).astype(BF16)
-    store(gk_o, gk_h)
-    store(gv_o, gv_h)
     for z in zpeers:
         arrived(zg.at[z], y_ss.at[z], y_rs.at[z], {"chan": z})
     for h in range(per):
@@ -410,12 +400,10 @@
         for z in zpeers:
             acc += zg[z, h].astype(F32)
         gf_o[:, h * w:(h + 1) * w] = acc
-    store(gf_o, gf_h)
     for q in senders:
         arrived(k_recv.at[q], k_ss.at[q], k_rs.at[q], {"seq": q})
     for q in range(n):
         gs_o[:, q * w:(q + 1) * w] = k_recv[q, 0:1]
-    store(gs_o, gs_h)
     for q in [me] + senders:
         at = lane(q)
         gain = skip[:, at]
@@ -423,24 +411,16 @@
             arrived(c_recv.at[2, q], c_ss.at[2, q], c_rs.at[2, q], {"seq": q})
         mixed = c_recv[2, q].astype(F32) + gain * s1_send[q].astype(F32)
         out_o[:, at] = (fq[:, at].astype(F32) * mixed).astype(BF16)
-    store(out_o, out_h)
     for c in started:
         c.wait_send()
+
+
+def store_all(*refs):
+    count = len(refs) // 2
+    near, far, sems = refs[:count], refs[count:2 * count], refs[-1]
+    stores = [pltpu.make_async_copy(near[i], far[i], sems.at[i]) for i in range(count)]
     for c in stores:
-        c.wait()
-
-
-def store_all(*refs):
-    count = len(refs) // 3
-    far, out, near = refs[:count], refs[count:2 * count], refs[2 * count:-1]
-    sems = refs[-1]
-    loads = [pltpu.make_async_copy(far[i], near[i], sems.at[0, i]) for i in range(count)]
-    stores = [pltpu.make_async_copy(near[i], out[i], sems.at[1, i]) for i in range(count)]
-    for c in loads:
         c.start()
-    for i in range(count):
-        loads[i].wait()
-        stores[i].start()
     for c in stores:
         c.wait()
 
@@ -452,10 +432,9 @@
     per = filters.shape[1] // w
     scale = 1.0 / math.sqrt(rows * n)
     forward, inverse = (jnp.asarray(t, dtype=BF16) for t in block_tables(rows))
-    wide = jax.ShapeDtypeStruct((rows, chan_width), BF16)
-    results = [
+    results = (
         *[pltpu.VMEM((rows, chan_width), BF16)] * 4, pltpu.VMEM(filters.shape, F32), pltpu.VMEM((1, chan_width), F32),
-    ]
+    )
     dma = pltpu.SemaphoreType.DMA
     block = (n, rows, w)
     spectrum = (n, 2 * rows, w)
@@ -463,7 +442,6 @@
         *[pltpu.VMEM((rows, chan_width), BF16)] * 7, pltpu.VMEM(filters.shape, F32),
         pltpu.VMEM((1, chan_width), F32), pltpu.VMEM(forward.shape, BF16), pltpu.VMEM(inverse.shape, BF16),
         dma((11,)),
-        *results, dma((6,)),
         pltpu.VMEM((n, 2, rows, w), BF16), pltpu.VMEM(block, BF16), pltpu.VMEM(block, BF16),
         pltpu.VMEM((n, 2, rows, w), BF16), pltpu.VMEM(block, BF16), pltpu.VMEM(block, BF16),
         *[pltpu.VMEM(spectrum, F32)] * 5,
@@ -473,28 +451,25 @@
         dma((n,)), dma((n,)), dma((n,)), dma((n,)), dma((n,)), dma((n,)), dma((nc,)), dma((nc,)),
         dma((3, n)), dma((3, n)), dma((n,)), dma((n,)), dma((nc,)), dma((nc,)), dma((n,)), dma((n,)),
     ]
-    full = 67_000_000
-    hbm = pl.BlockSpec(memory_space=pltpu.HBM)
+    operands = (*args[:8], skip.reshape(1, chan_width), forward, inverse)
+    hbm, vmem = (pl.BlockSpec(memory_space=m) for m in (pltpu.HBM, pltpu.VMEM))
     outs = pl.pallas_call(
         functools.partial(kernel, n, nc, scale),
-        out_shape=(
-            wide, wide, wide, wide,
-            jax.ShapeDtypeStruct(filters.shape, F32), jax.ShapeDtypeStruct((1, chan_width), F32),
-        ),
+        out_shape=results,
         in_specs=[hbm] * 11,
-        out_specs=(hbm,) * 6,
+        out_specs=(vmem,) * 6,
         scratch_shapes=scratch,
         compiler_params=pltpu.CompilerParams(
-            collective_id=0, has_side_effects=True, vmem_limit_bytes=full
+            collective_id=0, has_side_effects=True, vmem_limit_bytes=KERNEL_VMEM
         ),
-    )(*args[:8], skip.reshape(1, chan_width), forward, inverse)
+    )(*[pltpu.with_memory_space_constraint(a, pltpu.HBM) for a in operands])
     outs = pl.pallas_call(
         store_all,
         out_shape=tuple(jax.ShapeDtypeStruct(o.shape, o.dtype) for o in outs),
-        in_specs=[hbm] * 6,
+        in_specs=[vmem] * 6,
         out_specs=(hbm,) * 6,
-        scratch_shapes=[*results, dma((2, 6))],
-        compiler_params=pltpu.CompilerParams(vmem_limit_bytes=full),
+        scratch_shapes=[dma((6,))],
+        compiler_params=pltpu.CompilerParams(vmem_limit_bytes=KERNEL_VMEM),
     )(*outs)
     return tuple(outs[:5]) + (outs[5].reshape(chan_width),)
 

time: 36.9 us -> 35.2 us (0.954)
  Pallas kernels: 36.1 us -> 34.4 us
    pallas_call x1, Pallas kernels: 2.06 us -> 1.06 us  [fused_device(): pl.pallas_call(store_all, out_shape=tuple((jax.ShapeDtypeStruct(o.shape,...]
    pallas_call x1, Pallas kernels: 34 us -> 33.4 us  [fused_device(): pl.pallas_call(functools.partial(kernel, n, nc, scale), out_shape=results...]
where the time goes in v1:
time: 35.2 us; the launch traced here: 35.1 us
  Pallas kernels  34.4 us (98%)
  between operations  0.64 us (2%)
    pallas_call x1, Pallas kernels, fused_device(): pl.pallas_call(functools.partial(kernel, n, nc, scale), out_shape=results...  33.4 us
    pallas_call x1, Pallas kernels, fused_device(): pl.pallas_call(store_all, out_shape=tuple((jax.ShapeDtypeStruct(o.shape,...  1.06 us

profile of v1, /device:TPU:0, one launch (start us, length us, event | category | flops | bytes accessed | tf_op | source)
XLA Modules:
  0.0 35.1 jit_solution(6075803954052432907)
XLA Ops:
  0.6 33.4 %shard_map.154 = (bf16[128,1024]{1,0:T(8,128)(2,1)S(1)}, bf16[128,1024]{1,0:T(8,128)(2,1)S(1)}, bf16[128,1024]{1,0:T(8,128)(2,1)S(1)}, bf16[128,1024]{1,0:T(8,12...) custom-call(bf16[128,1024]{1,0:T(8,128)(2,1)} %fq_h.1, bf16[128,1024]{1,0:T(8,128)(2,1)} %fk_h.1, ...), custom_call_target="tpu_custom_call" | custom-call | tf_op jit(solution)/shard_map/pallas_call | solution.py:456
  34.0 1.1 %shard_map.155 = (bf16[128,1024]{1,0:T(8,128)(2,1)}, bf16[128,1024]{1,0:T(8,128)(2,1)}, bf16[128,1024]{1,0:T(8,128)(2,1)}, bf16[128,1024]{1,0:T(8,128)(2,1)}, f32[128,256]{1,0:T(8,128)}, /*index=5*/f32[1,1024]{1,0:T(1,128)}) custom-call(bf16[128,1024]{1,0:T(8,128)(2,1)S(1)} %get-tuple-element.18.refs_0_, bf16[128,1024]{1,0:T(8,128)(2,1)S(1)} %get-tuple-element.19.refs_1_, ...), custom_call_target="tpu_custom_call" | custom-call | tf_op jit(solution)/shard_map/pallas_call | solution.py:466

commit v2 on v1

--- a/solution.py
+++ b/solution.py
@@ -205,24 +205,44 @@
     return forward.astype(np.float32), inverse.astype(np.float32)
 
 
+REACH = 2
+
+
 def kernel(
     n, nc, scale,
     fq_h, fk_h, fv_h, bq_h, bk_h, bv_h, bg_h, filt_h, skip_h, fwd_h, inv_h,
     out_o, gq_o, gk_o, gv_o, gf_o, gs_o,
     fq, fk, fv, bq, bk, bv, bg, filt, skip, fwd_t, inv_t, in_sem,
     su_send, s1_send, fz, su, s1, rf, spec_s, spec_u, spec_f, spec_w, prod,
-    c_send, c_recv, g_send, rg, zg, k_send, k_recv,
-    su_ss, su_rs, s1_ss, s1_rs, f_ss, f_rs, z_ss, z_rs, c_ss, c_rs, g_ss, g_rs, y_ss, y_rs, k_ss, k_rs,
+    c_send, c_recv, g_send, zg, g2_send, g2_recv, g3, k_send, k_recv,
+    su_ss, su_rs, s1_ss, s1_rs, f_ss, f_rs, z_ss, z_rs, y_ss, c_ss, c_rs,
+    gz_ss, gz_rs, g2_ss, g2_rs, g3_ss, g3_rs, k_ss, k_rs,
 ):
     rows, chan_width = fq.shape
     w = chan_width // n
     per = filt.shape[1] // w
+    part, half = rows // nc, rows // 2
     me = lax.axis_index("seq")
     mz = lax.axis_index("chan")
-    peers = [lax.rem(me + r, n) for r in range(1, n)]
-    senders = peers[::-1]
-    zpeers = [lax.rem(mz + r, nc) for r in range(1, nc)]
-    started = []
+
+    def flipped(r):
+        at, bit = me, 1
+        while bit < n:
+            if r & bit:
+                at = at + bit * (1 - 2 * lax.rem(me // bit, 2))
+            bit *= 2
+        return at
+
+    order = sorted(range(1, n), key=lambda r: (r < 2, r & 1, -r))
+    peers = [flipped(r) for r in order]
+    upward = 2 * mz < nc
+    zorder = []
+    for k in range(nc - 1):
+        j = nc - 1 - k
+        zorder.append(jnp.where(upward, jnp.where(mz <= k, k + 1, k), jnp.where(mz >= j, j - 1, j)))
+
+    def near(z):
+        return (z - mz <= REACH) & (mz - z <= REACH)
 
     def lane(p):
         return pl.ds(pl.multiple_of(p * w, w), w)
@@ -232,6 +252,8 @@
             src_ref=src, dst_ref=dst, send_sem=ss, recv_sem=rs, device_id=to, device_id_type=MESH
         )
 
+    started = []
+
     def send(src, dst, ss, rs, to):
         c = copy(src, dst, ss, rs, to)
         c.start()
@@ -241,10 +263,10 @@
         copy(buf, buf, ss, rs, to).wait_recv()
 
     loads = {}
-    order = ((filt_h, filt), (bk_h, bk), (bv_h, bv), (bg_h, bg), (bq_h, bq), (fk_h, fk), (fv_h, fv))
-    for at, (far, near) in enumerate(order + ((fwd_h, fwd_t), (inv_h, inv_t), (skip_h, skip), (fq_h, fq))):
-        loads[id(near)] = pltpu.make_async_copy(far, near, in_sem.at[at])
-        loads[id(near)].start()
+    order_in = ((filt_h, filt), (bk_h, bk), (bv_h, bv), (bg_h, bg), (bq_h, bq), (fk_h, fk), (fv_h, fv))
+    for at, (far, dst) in enumerate(order_in + ((fwd_h, fwd_t), (inv_h, inv_t), (skip_h, skip), (fq_h, fq))):
+        loads[id(dst)] = pltpu.make_async_copy(far, dst, in_sem.at[at])
+        loads[id(dst)].start()
 
     def loaded(*refs):
         for ref in refs:
@@ -253,45 +275,86 @@
     barrier = pltpu.get_barrier_semaphore()
     for p in peers:
         pl.semaphore_signal(barrier, inc=1, device_id={"seq": p}, device_id_type=MESH)
-    for z in zpeers:
-        pl.semaphore_signal(barrier, inc=1, device_id={"chan": z}, device_id_type=MESH)
+    greeted = n - 1
+    for z in zorder:
+        greeted = greeted + near(z).astype(jnp.int32)
+
+        @pl.when(near(z))
+        def _(z=z):
+            pl.semaphore_signal(barrier, inc=1, device_id={"chan": z}, device_id_type=MESH)
 
     def transform(dst, q, block):
         dst[q] = jnp.dot(fwd_t[...], block, preferred_element_type=F32)
-
-    def gate_block(p):
-        at = lane(p)
-        su_send[p, 0] = (bk[:, at].astype(F32) * bv[:, at].astype(F32)).astype(BF16)
-        su_send[p, 1] = (bg[:, at].astype(F32) * bq[:, at].astype(F32)).astype(BF16)
 
     loaded(filt)
     for h in range(per):
         fz[mz * per + h] = filt[:, h * w:(h + 1) * w].astype(BF16)
-    pl.semaphore_wait(barrier, n - 1 + nc - 1)
-    for z in zpeers:
-        part = fz.at[pl.ds(mz * per, per)]
-        send(part, part, z_ss.at[z], z_rs.at[mz], {"chan": z})
     loaded(bk, bv, bg, bq)
+    for p in range(n):
+        cols = slice(p * w, (p + 1) * w)
+        su_send[p, 0] = (bk[:, cols].astype(F32) * bv[:, cols].astype(F32)).astype(BF16)
+        su_send[p, 1] = (bg[:, cols].astype(F32) * bq[:, cols].astype(F32)).astype(BF16)
+    pl.semaphore_wait(barrier, greeted)
+
+    def chan_copy(k, h):
+        block = fz.at[mz * per + h]
+        return copy(block, block, z_ss.at[k, h], z_rs.at[mz, h], {"chan": zorder[k]})
+
+    def relay_copy(o, h, to):
+        block = fz.at[o * per + h]
+        return copy(block, block, y_ss.at[h], z_rs.at[o, h], {"chan": to})
+
+    def forward(o, h):
+        p = o * per + h
+
+        @pl.when(p != me)
+        def _():
+            copy(fz.at[p], rf.at[me], f_ss.at[p], f_rs.at[me], {"seq": p}).start()
+
+    for k in range(nc - 2, -1, -1):
+        @pl.when(near(zorder[k]))
+        def _(k=k):
+            for h in range(per):
+                chan_copy(k, h).start()
+    for h in range(per):
+        forward(mz, h)
     for p in peers:
-        gate_block(p)
         send(su_send.at[p], su.at[me], su_ss.at[p], su_rs.at[me], {"seq": p})
-    gate_block(me)
-    su[me] = su_send[me]
+
     loaded(fk, fv)
     for p in range(n):
         cols = slice(p * w, (p + 1) * w)
         s1_send[p] = (fk[:, cols].astype(F32) * fv[:, cols].astype(F32)).astype(BF16)
+    su[me] = su_send[me]
     s1[me] = s1_send[me]
     loaded(fwd_t, inv_t)
     transform(spec_s, me, su[me, 0])
     transform(spec_u, me, su[me, 1])
-    for z in zpeers:
-        arrived(fz.at[pl.ds(z * per, per)], z_ss.at[z], z_rs.at[z], {"chan": z})
-    for p in peers:
-        send(fz.at[p], rf.at[me], f_ss.at[p], f_rs.at[me], {"seq": p})
-    for p in peers:
-        send(s1_send.at[p], s1.at[me], s1_ss.at[p], s1_rs.at[me], {"seq": p})
+
+    def send_s1(j):
+        piece = pl.ds(j * half, half)
+        for p in peers:
+            send(s1_send.at[p, piece], s1.at[me, piece], s1_ss.at[p, j], s1_rs.at[me, j], {"seq": p})
+
+    relays = []
+    for k in range(nc - 1):
+        o = zorder[k]
+        if k == nc - 2:
+            send_s1(0)
+            to = jnp.where(o > mz, mz - 1, mz + 1)
+            far = jnp.where(o > mz, o - mz, mz - o)
+            relays.append(((far == REACH) & (to >= 0) & (to < nc), o, to))
+        for h in range(per):
+            arrived(fz.at[o * per + h], z_ss.at[k, h], z_rs.at[o, h], {"chan": o})
+            for on, origin, to in relays:
+                @pl.when(on)
+                def _(origin=origin, to=to, h=h):
+                    relay_copy(origin, h, to).start()
+            forward(o, h)
     rf[me] = fz[me]
+    if nc == 1:
+        send_s1(0)
+    send_s1(1)
 
     sign = 1.0 - 2.0 * lax.rem(lax.broadcasted_iota(jnp.int32, (rows, w), 0), 2).astype(F32)
 
@@ -332,12 +395,17 @@
 
     def give_back(which):
         for p in peers:
+            send(c_send.at[which, p], c_recv.at[which, me], c_ss.at[which, p], c_rs.at[which, me], {"seq": p})
+
+    def outputs(which, now):
+        for p in peers:
             c_send[which, p] = inverse(p).astype(BF16)
-            send(c_send.at[which, p], c_recv.at[which, me], c_ss.at[which, p], c_rs.at[which, me], {"seq": p})
+            if now:
+                send(c_send.at[which, p], c_recv.at[which, me], c_ss.at[which, p], c_rs.at[which, me], {"seq": p})
         c_recv[which, me] = inverse(me).astype(BF16)
 
     total = jnp.zeros((1, w), F32)
-    for q in [me] + senders:
+    for q in [me] + peers:
         if q is not me:
             arrived(su.at[q], su_ss.at[q], su_rs.at[q], {"seq": q})
             transform(spec_s, q, su[q, 0])
@@ -350,42 +418,61 @@
 
     windowed(spec_s)
     products(spec_u, True)
-    for p in peers:
-        g_send[p] = (inverse(p) * scale).astype(BF16)
-        send(g_send.at[p], rg.at[me], g_ss.at[p], g_rs.at[me], {"seq": p})
-    rg[me] = (inverse(me) * scale).astype(BF16)
-
-    for q in [me] + senders:
+    for b in range(n):
+        g_send[b] = (inverse(b) * scale).astype(BF16)
+
+    def band(z):
+        return pl.ds(pl.multiple_of(z * part, part), part)
+
+    for k in range(nc - 2, -1, -1):
+        z = zorder[k]
+        send(g_send.at[:, band(z)], zg.at[mz], gz_ss.at[k], gz_rs.at[mz], {"chan": z})
+
+    for q in [me] + peers:
         if q is not me:
             arrived(rf.at[q], f_ss.at[q], f_rs.at[q], {"seq": q})
         transform(spec_f, q, rf[q])
     windowed(spec_f)
     products(spec_s, False)
-    give_back(0)
+    outputs(0, True)
     products(spec_u, True)
-    give_back(1)
-
-    for q in [me] + senders:
+    outputs(1, True)
+
+    for q in [me] + peers:
         if q is not me:
-            arrived(s1.at[q], s1_ss.at[q], s1_rs.at[q], {"seq": q})
+            for j in range(2):
+                piece = pl.ds(j * half, half)
+                arrived(s1.at[q, piece], s1_ss.at[q, j], s1_rs.at[q, j], {"seq": q})
         transform(spec_s, q, s1[q])
     products(spec_s, False)
+    outputs(2, False)
+
+    for k in range(nc - 1):
+        z = zorder[k]
+        arrived(zg.at[z], gz_ss.at[k], gz_rs.at[z], {"chan": z})
+    for p in range(n):
+        acc = g_send[p, band(mz)].astype(F32)
+        for z in zorder:
+            acc += zg[z, p].astype(F32)
+        g2_send[p] = acc.astype(BF16)
+    for p in peers:
+        send(g2_send.at[p], g2_recv.at[me], g2_ss.at[p], g2_rs.at[me], {"seq": p})
+    g2_recv[me] = g2_send[me]
     give_back(2)
 
-    for q in senders:
-        arrived(rg.at[q], g_ss.at[q], g_rs.at[q], {"seq": q})
-    for z in zpeers:
-        send(rg.at[pl.ds(z * per, per)], zg.at[mz], y_ss.at[z], y_rs.at[mz], {"chan": z})
-
     loaded(skip, fq)
-    for q in [me] + senders:
+    for q in [me] + peers:
         at = lane(q)
         gain = skip[:, at]
         if q is not me:
             arrived(c_recv.at[0, q], c_ss.at[0, q], c_rs.at[0, q], {"seq": q})
         mixed = c_recv[0, q].astype(F32) + gain * su_send[q, 0].astype(F32)
         gq_o[:, at] = (bg[:, at].astype(F32) * mixed).astype(BF16)
-    for q in [me] + senders:
+    for q in peers:
+        arrived(k_recv.at[q], k_ss.at[q], k_rs.at[q], {"seq": q})
+    for q in range(n):
+        gs_o[:, q * w:(q + 1) * w] = k_recv[q, 0:1]
+    for q in [me] + peers:
         at = lane(q)
         gain = skip[:, at]
         if q is not me:
@@ -393,26 +480,41 @@
         through = c_recv[1, q].astype(F32) + gain * su_send[q, 1].astype(F32)
         gk_o[:, at] = (through * bv[:, at].astype(F32)).astype(BF16)
         gv_o[:, at] = (through * bk[:, at].astype(F32)).astype(BF16)
-    for z in zpeers:
-        arrived(zg.at[z], y_ss.at[z], y_rs.at[z], {"chan": z})
+    for q in peers:
+        arrived(g2_recv.at[q], g2_ss.at[q], g2_rs.at[q], {"seq": q})
+    for k in range(nc - 2, -1, -1):
+        z = zorder[k]
+        send(g2_recv.at[pl.ds(z * per, per)], g3.at[mz], g3_ss.at[k], g3_rs.at[mz], {"chan": z})
     for h in range(per):
-        acc = rg[mz * per + h].astype(F32)
-        for z in zpeers:
-            acc += zg[z, h].astype(F32)
-        gf_o[:, h * w:(h + 1) * w] = acc
-    for q in senders:
-        arrived(k_recv.at[q], k_ss.at[q], k_rs.at[q], {"seq": q})
-    for q in range(n):
-        gs_o[:, q * w:(q + 1) * w] = k_recv[q, 0:1]
-    for q in [me] + senders:
+        g3[mz, h] = g2_recv[mz * per + h]
+    for q in [me] + peers:
         at = lane(q)
         gain = skip[:, at]
         if q is not me:
             arrived(c_recv.at[2, q], c_ss.at[2, q], c_rs.at[2, q], {"seq": q})
         mixed = c_recv[2, q].astype(F32) + gain * s1_send[q].astype(F32)
         out_o[:, at] = (fq[:, at].astype(F32) * mixed).astype(BF16)
+    for k in range(nc - 1):
+        z = zorder[k]
+        arrived(g3.at[z], g3_ss.at[k], g3_rs.at[z], {"chan": z})
+    for z in range(nc):
+        for h in range(per):
+            gf_o[z * part:(z + 1) * part, h * w:(h + 1) * w] = g3[z, h].astype(F32)
+
     for c in started:
         c.wait_send()
+    for p in peers:
+        copy(fz.at[p], rf.at[me], f_ss.at[p], f_rs.at[me], {"seq": p}).wait_send()
+    for k in range(nc - 1):
+        @pl.when(near(zorder[k]))
+        def _(k=k):
+            for h in range(per):
+                chan_copy(k, h).wait_send()
+    for on, origin, to in relays:
+        @pl.when(on)
+        def _(origin=origin, to=to):
+            for h in range(per):
+                relay_copy(origin, h, to).wait_send()
 
 
 def store_all(*refs):
@@ -430,6 +532,7 @@
     rows, chan_width = fwd_q.shape
     w = chan_width // n
     per = filters.shape[1] // w
+    part = rows // nc
     scale = 1.0 / math.sqrt(rows * n)
     forward, inverse = (jnp.asarray(t, dtype=BF16) for t in block_tables(rows))
     results = (
@@ -446,10 +549,12 @@
         pltpu.VMEM((n, 2, rows, w), BF16), pltpu.VMEM(block, BF16), pltpu.VMEM(block, BF16),
         *[pltpu.VMEM(spectrum, F32)] * 5,
         pltpu.VMEM((3,) + block, BF16), pltpu.VMEM((3,) + block, BF16),
-        pltpu.VMEM(block, BF16), pltpu.VMEM(block, BF16), pltpu.VMEM((nc, per, rows, w), BF16),
+        pltpu.VMEM(block, BF16), pltpu.VMEM((nc, n, part, w), BF16),
+        pltpu.VMEM((n, part, w), BF16), pltpu.VMEM((n, part, w), BF16), pltpu.VMEM((nc, per, part, w), BF16),
         pltpu.VMEM((8, w), F32), pltpu.VMEM((n, 8, w), F32),
-        dma((n,)), dma((n,)), dma((n,)), dma((n,)), dma((n,)), dma((n,)), dma((nc,)), dma((nc,)),
-        dma((3, n)), dma((3, n)), dma((n,)), dma((n,)), dma((nc,)), dma((nc,)), dma((n,)), dma((n,)),
+        dma((n,)), dma((n,)), dma((n, 2)), dma((n, 2)), dma((n,)), dma((n,)),
+        dma((nc, per)), dma((nc, per)), dma((per,)), dma((3, n)), dma((3, n)),
+        dma((nc,)), dma((nc,)), dma((n,)), dma((n,)), dma((nc,)), dma((nc,)), dma((n,)), dma((n,)),
     ]
     operands = (*args[:8], skip.reshape(1, chan_width), forward, inverse)
     hbm, vmem = (pl.BlockSpec(memory_space=m) for m in (pltpu.HBM, pltpu.VMEM))
@@ -478,7 +583,8 @@
     n, nc = lax.axis_size("seq"), lax.axis_size("chan")
     rows, chan_width = args[0].shape
     filter_width = args[7].shape[1]
-    fits = chan_width % (n * LANES) == 0 and rows % 16 == 0
+    fits = chan_width % (n * LANES) == 0 and rows % (16 * nc) == 0 and rows % 32 == 0
+    fits = fits and n & (n - 1) == 0 and nc <= REACH + 2
     if fits and filter_width * nc == chan_width and filter_width % (chan_width // n) == 0:
         return fused_device(n, nc, *args)
     return per_device(*args)

time: 35.2 us -> 36.4 us (1.034)
  Pallas kernels: 34.4 us -> 35.6 us
    pallas_call x1, Pallas kernels: 33.4 us -> 34.5 us  [fused_device(): pl.pallas_call(functools.partial(kernel, n, nc, scale), out_shape=results...]
where the time goes in v2:
time: 36.4 us; the launch traced here: 36.2 us
  Pallas kernels  35.6 us (98%)
  between operations  0.64 us (2%)
    pallas_call x1, Pallas kernels, fused_device(): pl.pallas_call(functools.partial(kernel, n, nc, scale), out_shape=results...  34.5 us
    pallas_call x1, Pallas kernels, fused_device(): pl.pallas_call(store_all, out_shape=tuple((jax.ShapeDtypeStruct(o.shape,...  1.06 us

profile of v2, /device:TPU:0, one launch (start us, length us, event | category | flops | bytes accessed | tf_op | source)
XLA Modules:
  0.0 36.2 jit_solution(9386292137070407388)
XLA Ops:
  0.6 34.5 %shard_map.154 = (bf16[128,1024]{1,0:T(8,128)(2,1)S(1)}, bf16[128,1024]{1,0:T(8,128)(2,1)S(1)}, bf16[128,1024]{1,0:T(8,128)(2,1)S(1)}, bf16[128,1024]{1,0:T(8,12...) custom-call(bf16[128,1024]{1,0:T(8,128)(2,1)} %fq_h.1, bf16[128,1024]{1,0:T(8,128)(2,1)} %fk_h.1, ...), custom_call_target="tpu_custom_call" | custom-call | tf_op jit(solution)/shard_map/pallas_call | solution.py:561
  35.2 1.1 %shard_map.155 = (bf16[128,1024]{1,0:T(8,128)(2,1)}, bf16[128,1024]{1,0:T(8,128)(2,1)}, bf16[128,1024]{1,0:T(8,128)(2,1)}, bf16[128,1024]{1,0:T(8,128)(2,1)}, f32[128,256]{1,0:T(8,128)}, /*index=5*/f32[1,1024]{1,0:T(1,128)}) custom-call(bf16[128,1024]{1,0:T(8,128)(2,1)S(1)} %get-tuple-element.18.refs_0_, bf16[128,1024]{1,0:T(8,128)(2,1)S(1)} %get-tuple-element.19.refs_1_, ...), custom_call_target="tpu_custom_call" | custom-call | tf_op jit(solution)/shard_map/pallas_call | solution.py:571

commit v3 on v2

--- a/solution.py
+++ b/solution.py
@@ -215,7 +215,7 @@
     fq, fk, fv, bq, bk, bv, bg, filt, skip, fwd_t, inv_t, in_sem,
     su_send, s1_send, fz, su, s1, rf, spec_s, spec_u, spec_f, spec_w, prod,
     c_send, c_recv, g_send, zg, g2_send, g2_recv, g3, k_send, k_recv,
-    su_ss, su_rs, s1_ss, s1_rs, f_ss, f_rs, z_ss, z_rs, y_ss, c_ss, c_rs,
+    su_ss, su_rs, s1_ss, s1_rs, f_ss, f_rs, z_ss, z_rs, credit, c_ss, c_rs,
     gz_ss, gz_rs, g2_ss, g2_rs, g3_ss, g3_rs, k_ss, k_rs,
 ):
     rows, chan_width = fq.shape
@@ -233,7 +233,7 @@
             bit *= 2
         return at
 
-    order = sorted(range(1, n), key=lambda r: (r < 2, r & 1, -r))
+    order = sorted(range(1, n), key=lambda r: (r & 1, -r))
     peers = [flipped(r) for r in order]
     upward = 2 * mz < nc
     zorder = []
@@ -300,10 +300,6 @@
         block = fz.at[mz * per + h]
         return copy(block, block, z_ss.at[k, h], z_rs.at[mz, h], {"chan": zorder[k]})
 
-    def relay_copy(o, h, to):
-        block = fz.at[o * per + h]
-        return copy(block, block, y_ss.at[h], z_rs.at[o, h], {"chan": to})
-
     def forward(o, h):
         p = o * per + h
 
@@ -311,15 +307,34 @@
         def _():
             copy(fz.at[p], rf.at[me], f_ss.at[p], f_rs.at[me], {"seq": p}).start()
 
-    for k in range(nc - 2, -1, -1):
-        @pl.when(near(zorder[k]))
-        def _(k=k):
-            for h in range(per):
-                chan_copy(k, h).start()
+    def chan_send(k):
+        for h in range(per):
+            chan_copy(k, h).start()
+
+    distant = ~near(zorder[-1]) if nc > 1 else None
+    if nc > 1:
+        o = zorder[-1]
+        other = jnp.where(o > mz, mz - 1, mz + 1)
+        vouch = ((o - mz == REACH) | (mz - o == REACH)) & (other >= 0) & (other < nc)
+
+        @pl.when(vouch)
+        def _():
+            pl.semaphore_signal(credit, inc=1, device_id={"chan": o}, device_id_type=MESH)
+
+        @pl.when(~distant)
+        def _():
+            for k in range(nc - 2, -1, -1):
+                chan_send(k)
+
+        @pl.when(distant)
+        def _():
+            for k in range(nc - 3, 0, -1):
+                chan_send(k)
+
+    for p in peers:
+        send(su_send.at[p], su.at[me], su_ss.at[p], su_rs.at[me], {"seq": p})
     for h in range(per):
         forward(mz, h)
-    for p in peers:
-        send(su_send.at[p], su.at[me], su_ss.at[p], su_rs.at[me], {"seq": p})
 
     loaded(fk, fv)
     for p in range(n):
@@ -331,30 +346,21 @@
     transform(spec_s, me, su[me, 0])
     transform(spec_u, me, su[me, 1])
 
-    def send_s1(j):
-        piece = pl.ds(j * half, half)
-        for p in peers:
-            send(s1_send.at[p, piece], s1.at[me, piece], s1_ss.at[p, j], s1_rs.at[me, j], {"seq": p})
-
-    relays = []
+    if nc > 1:
+        @pl.when(distant)
+        def _():
+            pl.semaphore_wait(credit, 1)
+            chan_send(nc - 2)
+            chan_send(0)
+
     for k in range(nc - 1):
         o = zorder[k]
-        if k == nc - 2:
-            send_s1(0)
-            to = jnp.where(o > mz, mz - 1, mz + 1)
-            far = jnp.where(o > mz, o - mz, mz - o)
-            relays.append(((far == REACH) & (to >= 0) & (to < nc), o, to))
         for h in range(per):
             arrived(fz.at[o * per + h], z_ss.at[k, h], z_rs.at[o, h], {"chan": o})
-            for on, origin, to in relays:
-                @pl.when(on)
-                def _(origin=origin, to=to, h=h):
-                    relay_copy(origin, h, to).start()
             forward(o, h)
     rf[me] = fz[me]
-    if nc == 1:
-        send_s1(0)
-    send_s1(1)
+    for p in peers:
+        send(s1_send.at[p], s1.at[me], s1_ss.at[p], s1_rs.at[me], {"seq": p})
 
     sign = 1.0 - 2.0 * lax.rem(lax.broadcasted_iota(jnp.int32, (rows, w), 0), 2).astype(F32)
 
@@ -393,23 +399,28 @@
     def inverse(b):
         return jnp.dot(inv_t[...], prod[b].astype(BF16), preferred_element_type=F32)
 
-    def give_back(which):
-        for p in peers:
+    def batches(items):
+        return [items[:n // 2], items[n // 2:]]
+
+    def give_back(which, group):
+        for p in group:
             send(c_send.at[which, p], c_recv.at[which, me], c_ss.at[which, p], c_rs.at[which, me], {"seq": p})
 
     def outputs(which, now):
-        for p in peers:
-            c_send[which, p] = inverse(p).astype(BF16)
-            if now:
-                send(c_send.at[which, p], c_recv.at[which, me], c_ss.at[which, p], c_rs.at[which, me], {"seq": p})
+        for group in batches(peers):
+            for p in group:
+                c_send[which, p] = inverse(p).astype(BF16)
+            give_back(which, [p for p in group if any(p is x for x in now)])
         c_recv[which, me] = inverse(me).astype(BF16)
 
-    total = jnp.zeros((1, w), F32)
-    for q in [me] + peers:
-        if q is not me:
+    for group in batches(peers):
+        for q in group:
             arrived(su.at[q], su_ss.at[q], su_rs.at[q], {"seq": q})
+        for q in group:
             transform(spec_s, q, su[q, 0])
             transform(spec_u, q, su[q, 1])
+    total = jnp.zeros((1, w), F32)
+    for q in range(n):
         total += jnp.sum(su[q, 0].astype(F32) * su[q, 1].astype(F32), axis=0, keepdims=True)
     k_send[...] = jnp.broadcast_to(total * scale, k_send.shape)
     for p in peers:
@@ -428,24 +439,24 @@
         z = zorder[k]
         send(g_send.at[:, band(z)], zg.at[mz], gz_ss.at[k], gz_rs.at[mz], {"chan": z})
 
-    for q in [me] + peers:
-        if q is not me:
+    transform(spec_f, me, rf[me])
+    for group in batches(peers):
+        for q in group:
             arrived(rf.at[q], f_ss.at[q], f_rs.at[q], {"seq": q})
-        transform(spec_f, q, rf[q])
+        for q in group:
+            transform(spec_f, q, rf[q])
     windowed(spec_f)
     products(spec_s, False)
-    outputs(0, True)
+    outputs(0, peers)
     products(spec_u, True)
-    outputs(1, True)
-
-    for q in [me] + peers:
-        if q is not me:
-            for j in range(2):
-                piece = pl.ds(j * half, half)
-                arrived(s1.at[q, piece], s1_ss.at[q, j], s1_rs.at[q, j], {"seq": q})
+    outputs(1, batches(peers)[0])
+
+    for q in peers:
+        arrived(s1.at[q], s1_ss.at[q], s1_rs.at[q], {"seq": q})
+    for q in range(n):
         transform(spec_s, q, s1[q])
     products(spec_s, False)
-    outputs(2, False)
+    outputs(2, [])
 
     for k in range(nc - 1):
         z = zorder[k]
@@ -458,7 +469,8 @@
     for p in peers:
         send(g2_send.at[p], g2_recv.at[me], g2_ss.at[p], g2_rs.at[me], {"seq": p})
     g2_recv[me] = g2_send[me]
-    give_back(2)
+    give_back(1, batches(peers)[1])
+    give_back(2, peers)
 
     loaded(skip, fq)
     for q in [me] + peers:
@@ -468,6 +480,13 @@
             arrived(c_recv.at[0, q], c_ss.at[0, q], c_rs.at[0, q], {"seq": q})
         mixed = c_recv[0, q].astype(F32) + gain * su_send[q, 0].astype(F32)
         gq_o[:, at] = (bg[:, at].astype(F32) * mixed).astype(BF16)
+    for q in peers:
+        arrived(g2_recv.at[q], g2_ss.at[q], g2_rs.at[q], {"seq": q})
+    for k in range(nc - 2, -1, -1):
+        z = zorder[k]
+        send(g2_recv.at[pl.ds(z * per, per)], g3.at[mz], g3_ss.at[k], g3_rs.at[mz], {"chan": z})
+    for h in range(per):
+        g3[mz, h] = g2_recv[mz * per + h]
     for q in peers:
         arrived(k_recv.at[q], k_ss.at[q], k_rs.at[q], {"seq": q})
     for q in range(n):
@@ -480,13 +499,6 @@
         through = c_recv[1, q].astype(F32) + gain * su_send[q, 1].astype(F32)
         gk_o[:, at] = (through * bv[:, at].astype(F32)).astype(BF16)
         gv_o[:, at] = (through * bk[:, at].astype(F32)).astype(BF16)
-    for q in peers:
-        arrived(g2_recv.at[q], g2_ss.at[q], g2_rs.at[q], {"seq": q})
-    for k in range(nc - 2, -1, -1):
-        z = zorder[k]
-        send(g2_recv.at[pl.ds(z * per, per)], g3.at[mz], g3_ss.at[k], g3_rs.at[mz], {"chan": z})
-    for h in range(per):
-        g3[mz, h] = g2_recv[mz * per + h]
     for q in [me] + peers:
         at = lane(q)
         gain = skip[:, at]
@@ -506,15 +518,8 @@
     for p in peers:
         copy(fz.at[p], rf.at[me], f_ss.at[p], f_rs.at[me], {"seq": p}).wait_send()
     for k in range(nc - 1):
-        @pl.when(near(zorder[k]))
-        def _(k=k):
-            for h in range(per):
-                chan_copy(k, h).wait_send()
-    for on, origin, to in relays:
-        @pl.when(on)
-        def _(origin=origin, to=to):
-            for h in range(per):
-                relay_copy(origin, h, to).wait_send()
+        for h in range(per):
+            chan_copy(k, h).wait_send()
 
 
 def store_all(*refs):
@@ -552,8 +557,8 @@
         pltpu.VMEM(block, BF16), pltpu.VMEM((nc, n, part, w), BF16),
         pltpu.VMEM((n, part, w), BF16), pltpu.VMEM((n, part, w), BF16), pltpu.VMEM((nc, per, part, w), BF16),
         pltpu.VMEM((8, w), F32), pltpu.VMEM((n, 8, w), F32),
-        dma((n,)), dma((n,)), dma((n, 2)), dma((n, 2)), dma((n,)), dma((n,)),
-        dma((nc, per)), dma((nc, per)), dma((per,)), dma((3, n)), dma((3, n)),
+        dma((n,)), dma((n,)), dma((n,)), dma((n,)), dma((n,)), dma((n,)),
+        dma((nc, per)), dma((nc, per)), pltpu.SemaphoreType.REGULAR, dma((3, n)), dma((3, n)),
         dma((nc,)), dma((nc,)), dma((n,)), dma((n,)), dma((nc,)), dma((nc,)), dma((n,)), dma((n,)),
     ]
     operands = (*args[:8], skip.reshape(1, chan_width), forward, inverse)

time: 36.4 us -> 33.9 us (0.931)
  Pallas kernels: 35.6 us -> 33.1 us
    pallas_call x1, Pallas kernels: 34.5 us -> 32 us  [fused_device(): pl.pallas_call(functools.partial(kernel, n, nc, scale), out_shape=results...]
where the time goes in v3:
time: 33.9 us; the launch traced here: 33.7 us
  Pallas kernels  33.1 us (98%)
  between operations  0.64 us (2%)
    pallas_call x1, Pallas kernels, fused_device(): pl.pallas_call(functools.partial(kernel, n, nc, scale), out_shape=results...  32 us
    pallas_call x1, Pallas kernels, fused_device(): pl.pallas_call(store_all, out_shape=tuple((jax.ShapeDtypeStruct(o.shape,...  1.06 us

profile of v3, /device:TPU:0, one launch (start us, length us, event | category | flops | bytes accessed | tf_op | source)
XLA Modules:
  0.0 33.7 jit_solution(7551680929636424359)
XLA Ops:
  0.6 32.0 %shard_map.154 = (bf16[128,1024]{1,0:T(8,128)(2,1)S(1)}, bf16[128,1024]{1,0:T(8,128)(2,1)S(1)}, bf16[128,1024]{1,0:T(8,128)(2,1)S(1)}, bf16[128,1024]{1,0:T(8,12...) custom-call(bf16[128,1024]{1,0:T(8,128)(2,1)} %fq_h.1, bf16[128,1024]{1,0:T(8,128)(2,1)} %fk_h.1, ...), custom_call_target="tpu_custom_call" | custom-call | tf_op jit(solution)/shard_map/pallas_call | solution.py:566
  32.7 1.1 %shard_map.155 = (bf16[128,1024]{1,0:T(8,128)(2,1)}, bf16[128,1024]{1,0:T(8,128)(2,1)}, bf16[128,1024]{1,0:T(8,128)(2,1)}, bf16[128,1024]{1,0:T(8,128)(2,1)}, f32[128,256]{1,0:T(8,128)}, /*index=5*/f32[1,1024]{1,0:T(1,128)}) custom-call(bf16[128,1024]{1,0:T(8,128)(2,1)S(1)} %get-tuple-element.18.refs_0_, bf16[128,1024]{1,0:T(8,128)(2,1)S(1)} %get-tuple-element.19.refs_1_, ...), custom_call_target="tpu_custom_call" | custom-call | tf_op jit(solution)/shard_map/pallas_call | solution.py:576

commit v4 on v3

--- a/solution.py
+++ b/solution.py
@@ -213,9 +213,9 @@
     fq_h, fk_h, fv_h, bq_h, bk_h, bv_h, bg_h, filt_h, skip_h, fwd_h, inv_h,
     out_o, gq_o, gk_o, gv_o, gf_o, gs_o,
     fq, fk, fv, bq, bk, bv, bg, filt, skip, fwd_t, inv_t, in_sem,
-    su_send, s1_send, fz, su, s1, rf, spec_s, spec_u, spec_f, spec_w, prod,
+    s2_send, up_send, s1_send, fz, s2, up, s1, rf, spec_s, spec_u, spec_f, spec_w, prod,
     c_send, c_recv, g_send, zg, g2_send, g2_recv, g3, k_send, k_recv,
-    su_ss, su_rs, s1_ss, s1_rs, f_ss, f_rs, z_ss, z_rs, credit, c_ss, c_rs,
+    in_ss, s2_rs, up_rs, s1_rs, f_ss, f_rs, z_ss, z_rs, credit, c_ss, c_rs,
     gz_ss, gz_rs, g2_ss, g2_rs, g3_ss, g3_rs, k_ss, k_rs,
 ):
     rows, chan_width = fq.shape
@@ -235,6 +235,7 @@
 
     order = sorted(range(1, n), key=lambda r: (r & 1, -r))
     peers = [flipped(r) for r in order]
+    paired = list(zip(order, peers))
     upward = 2 * mz < nc
     zorder = []
     for k in range(nc - 1):
@@ -252,18 +253,25 @@
             src_ref=src, dst_ref=dst, send_sem=ss, recv_sem=rs, device_id=to, device_id_type=MESH
         )
 
-    started = []
-
     def send(src, dst, ss, rs, to):
-        c = copy(src, dst, ss, rs, to)
-        c.start()
-        started.append(c)
-
-    def arrived(buf, ss, rs, to):
-        copy(buf, buf, ss, rs, to).wait_recv()
+        copy(src, dst, ss, rs, to).start()
+
+    def arrived(buf, rs):
+        copy(buf, buf, rs, rs, {"seq": peers[0]}).wait_recv()
+
+    def sent(buf, ss):
+        copy(buf, buf, ss, ss, {"seq": peers[0]}).wait_send()
+
+    span, count = 2 * rows, n // 2
+    near_side = 2 * (count // 2)
+
+    def side(r):
+        return 1 if r >= near_side else 0
+
+    offsets = (range(1, near_side), range(max(near_side, 1), n))
 
     loads = {}
-    order_in = ((filt_h, filt), (bk_h, bk), (bv_h, bv), (bg_h, bg), (bq_h, bq), (fk_h, fk), (fv_h, fv))
+    order_in = ((bk_h, bk), (bv_h, bv), (filt_h, filt), (bg_h, bg), (bq_h, bq), (fk_h, fk), (fv_h, fv))
     for at, (far, dst) in enumerate(order_in + ((fwd_h, fwd_t), (inv_h, inv_t), (skip_h, skip), (fq_h, fq))):
         loads[id(dst)] = pltpu.make_async_copy(far, dst, in_sem.at[at])
         loads[id(dst)].start()
@@ -283,33 +291,35 @@
         def _(z=z):
             pl.semaphore_signal(barrier, inc=1, device_id={"chan": z}, device_id_type=MESH)
 
-    def transform(dst, q, block):
-        dst[q] = jnp.dot(fwd_t[...], block, preferred_element_type=F32)
-
+    chips = [flipped(r) // 2 for r in range(n - 2, 0, -2)] + [me // 2]
+
+    def transform(dst, c, src):
+        block = jnp.concatenate([src[2 * c], src[2 * c + 1]], axis=0)
+        dst[c] = jnp.dot(fwd_t[...], block, preferred_element_type=F32)
+
+    def gated(dst, left, right):
+        for p in range(n):
+            cols = slice(p * w, (p + 1) * w)
+            dst[p] = (left[:, cols].astype(F32) * right[:, cols].astype(F32)).astype(BF16)
+
+    loaded(bk, bv)
+    gated(s2_send, bk, bv)
     loaded(filt)
     for h in range(per):
         fz[mz * per + h] = filt[:, h * w:(h + 1) * w].astype(BF16)
-    loaded(bk, bv, bg, bq)
-    for p in range(n):
-        cols = slice(p * w, (p + 1) * w)
-        su_send[p, 0] = (bk[:, cols].astype(F32) * bv[:, cols].astype(F32)).astype(BF16)
-        su_send[p, 1] = (bg[:, cols].astype(F32) * bq[:, cols].astype(F32)).astype(BF16)
     pl.semaphore_wait(barrier, greeted)
-
-    def chan_copy(k, h):
-        block = fz.at[mz * per + h]
-        return copy(block, block, z_ss.at[k, h], z_rs.at[mz, h], {"chan": zorder[k]})
 
     def forward(o, h):
         p = o * per + h
 
         @pl.when(p != me)
         def _():
-            copy(fz.at[p], rf.at[me], f_ss.at[p], f_rs.at[me], {"seq": p}).start()
+            away = jnp.where(p // near_side == me // near_side, 0, 1) if near_side else 1
+            send(fz.at[p], rf.at[me], f_ss, f_rs.at[away], {"seq": p})
 
     def chan_send(k):
-        for h in range(per):
-            chan_copy(k, h).start()
+        block = fz.at[pl.ds(mz * per, per)]
+        send(block, block, z_ss, z_rs.at[mz], {"chan": zorder[k]})
 
     distant = ~near(zorder[-1]) if nc > 1 else None
     if nc > 1:
@@ -328,58 +338,57 @@
 
         @pl.when(distant)
         def _():
-            for k in range(nc - 3, 0, -1):
+            for k in range(nc - 3, -1, -1):
                 chan_send(k)
 
-    for p in peers:
-        send(su_send.at[p], su.at[me], su_ss.at[p], su_rs.at[me], {"seq": p})
-    for h in range(per):
-        forward(mz, h)
-
+    def scatter(src, dst, ss, rs):
+        for r, p in paired:
+            send(src.at[p], dst.at[me], ss, rs.at[side(r)], {"seq": p})
+        dst[me] = src[me]
+
+    scatter(s2_send, s2, in_ss, s2_rs)
+    loaded(bg, bq)
+    gated(up_send, bg, bq)
+    scatter(up_send, up, in_ss, up_rs)
     loaded(fk, fv)
-    for p in range(n):
-        cols = slice(p * w, (p + 1) * w)
-        s1_send[p] = (fk[:, cols].astype(F32) * fv[:, cols].astype(F32)).astype(BF16)
-    su[me] = su_send[me]
-    s1[me] = s1_send[me]
+    gated(s1_send, fk, fv)
     loaded(fwd_t, inv_t)
-    transform(spec_s, me, su[me, 0])
-    transform(spec_u, me, su[me, 1])
 
     if nc > 1:
         @pl.when(distant)
         def _():
             pl.semaphore_wait(credit, 1)
             chan_send(nc - 2)
-            chan_send(0)
 
     for k in range(nc - 1):
         o = zorder[k]
+        arrived(fz.at[pl.ds(o * per, per)], z_rs.at[o])
         for h in range(per):
-            arrived(fz.at[o * per + h], z_ss.at[k, h], z_rs.at[o, h], {"chan": o})
+            if k == 0:
+                forward(mz, h)
             forward(o, h)
+    for h in range(per if nc == 1 else 0):
+        forward(mz, h)
     rf[me] = fz[me]
-    for p in peers:
-        send(s1_send.at[p], s1.at[me], s1_ss.at[p], s1_rs.at[me], {"seq": p})
-
-    sign = 1.0 - 2.0 * lax.rem(lax.broadcasted_iota(jnp.int32, (rows, w), 0), 2).astype(F32)
+
+    sign = 1.0 - 2.0 * lax.rem(lax.broadcasted_iota(jnp.int32, (span, w), 0), 2).astype(F32)
 
     def windowed(src):
         spec_w[0] = src[0]
-        for d in range(1, n):
-            spec_w[d, :rows] = src[d, :rows] - sign * src[d - 1, rows:]
-            spec_w[d, rows:] = src[d, rows:] + sign * src[d - 1, :rows]
+        for d in range(1, count):
+            spec_w[d, :span] = src[d, :span] - sign * src[d - 1, span:]
+            spec_w[d, span:] = src[d, span:] + sign * src[d - 1, :span]
 
     def products(src, corr):
         def tile(k, carry):
-            re_at = pl.ds(pl.multiple_of(k * 8, 8), 8)
-            im_at = pl.ds(pl.multiple_of(rows + k * 8, 8), 8)
-            ar = [spec_w[d, re_at] for d in range(n)]
-            ai = [spec_w[d, im_at] for d in range(n)]
-            xr = [src[d, re_at] for d in range(n)]
-            xi = [src[d, im_at] for d in range(n)]
-            for b in range(n):
-                terms = [(c - b, c) for c in range(b, n)] if corr else [(b - c, c) for c in range(b + 1)]
+            re_at = pl.ds(pl.multiple_of(k * 16, 16), 16)
+            im_at = pl.ds(pl.multiple_of(span + k * 16, 16), 16)
+            ar = [spec_w[d, re_at] for d in range(count)]
+            ai = [spec_w[d, im_at] for d in range(count)]
+            xr = [src[d, re_at] for d in range(count)]
+            xi = [src[d, im_at] for d in range(count)]
+            for b in range(count):
+                terms = [(c - b, c) for c in range(b, count)] if corr else [(b - c, c) for c in range(b + 1)]
                 re, im = None, None
                 for d, c in terms:
                     if corr:
@@ -394,132 +403,136 @@
                 prod[b, im_at] = im
             return carry
 
-        lax.fori_loop(0, rows // 8, tile, 0)
+        lax.fori_loop(0, span // 16, tile, 0)
 
     def inverse(b):
         return jnp.dot(inv_t[...], prod[b].astype(BF16), preferred_element_type=F32)
 
+    def give_back(which, group):
+        for r in group:
+            p = flipped(r)
+            send(c_send.at[which, p], c_recv.at[which, me], c_ss, c_rs.at[which, side(r)], {"seq": p})
+
+    def halves(dst, c, value):
+        dst[2 * c] = value[:rows].astype(BF16)
+        dst[2 * c + 1] = value[rows:].astype(BF16)
+
     def batches(items):
-        return [items[:n // 2], items[n // 2:]]
-
-    def give_back(which, group):
-        for p in group:
-            send(c_send.at[which, p], c_recv.at[which, me], c_ss.at[which, p], c_rs.at[which, me], {"seq": p})
+        return [items[:len(items) // 2], items[len(items) // 2:]]
 
     def outputs(which, now):
-        for group in batches(peers):
-            for p in group:
-                c_send[which, p] = inverse(p).astype(BF16)
-            give_back(which, [p for p in group if any(p is x for x in now)])
-        c_recv[which, me] = inverse(me).astype(BF16)
-
-    for group in batches(peers):
-        for q in group:
-            arrived(su.at[q], su_ss.at[q], su_rs.at[q], {"seq": q})
-        for q in group:
-            transform(spec_s, q, su[q, 0])
-            transform(spec_u, q, su[q, 1])
+        for group in batches(list(range(count))):
+            for i in group:
+                halves(c_send.at[which], chips[i], inverse(chips[i]))
+            if now:
+                give_back(which, [r for i in group for r in (n - 2 - 2 * i, n - 1 - 2 * i) if r])
+        c_recv[which, me] = c_send[which, me]
+
+    def gather(bufs, rs, specs):
+        for at, group in enumerate(batches(list(range(count))[::-1])):
+            for buf, sems in zip(bufs, rs):
+                if len(offsets[at]):
+                    arrived(buf.at[pl.ds(0, len(offsets[at]))], sems.at[at])
+            for buf, spec in zip(bufs, specs):
+                for i in group:
+                    transform(spec, chips[i], buf)
+
+    gather((s2, up), (s2_rs, up_rs), (spec_s, spec_u))
+    scatter(s1_send, s1, in_ss, s1_rs)
+    windowed(spec_s)
+    products(spec_u, True)
+    for b in range(count):
+        halves(g_send, b, inverse(b) * scale)
+
+    def place(z):
+        return jnp.where(mz > z, mz - 1, mz)
+
+    def band(z):
+        return pl.ds(pl.multiple_of(z * part, part), part)
+
+    for k in range(nc - 2, -1, -1):
+        z = zorder[k]
+        send(g_send.at[:, band(z)], zg.at[place(z)], gz_ss, gz_rs, {"chan": z})
+
     total = jnp.zeros((1, w), F32)
     for q in range(n):
-        total += jnp.sum(su[q, 0].astype(F32) * su[q, 1].astype(F32), axis=0, keepdims=True)
+        total += jnp.sum(s2[q].astype(F32) * up[q].astype(F32), axis=0, keepdims=True)
     k_send[...] = jnp.broadcast_to(total * scale, k_send.shape)
     for p in peers:
-        send(k_send, k_recv.at[me], k_ss.at[p], k_rs.at[me], {"seq": p})
+        send(k_send, k_recv.at[me], k_ss, k_rs, {"seq": p})
     k_recv[me] = k_send[...]
 
-    windowed(spec_s)
+    gather((rf,), (f_rs,), (spec_f,))
+    windowed(spec_f)
+    products(spec_s, False)
+    outputs(0, True)
     products(spec_u, True)
-    for b in range(n):
-        g_send[b] = (inverse(b) * scale).astype(BF16)
-
-    def band(z):
-        return pl.ds(pl.multiple_of(z * part, part), part)
-
+    outputs(1, False)
+    early, late = order[:n // 2], order[n // 2:]
+    give_back(1, early)
+
+    gather((s1,), (s1_rs,), (spec_s,))
+    products(spec_s, False)
+    outputs(2, False)
+
+    if nc > 1:
+        arrived(zg.at[pl.ds(0, nc - 1)], gz_rs)
+    for p in range(n):
+        acc = g_send[p, band(mz)].astype(F32)
+        for k in range(nc - 1):
+            acc += zg[k, p].astype(F32)
+        g2_send[p] = acc.astype(BF16)
+    for p in peers:
+        send(g2_send.at[p], g2_recv.at[me], g2_ss, g2_rs, {"seq": p})
+    g2_recv[me] = g2_send[me]
+    give_back(1, late)
+    give_back(2, order)
+
+    loaded(skip, fq)
+
+    def returned(which):
+        for at in range(2):
+            group = [flipped(r) for r in offsets[at]]
+            if group:
+                arrived(c_recv.at[which, pl.ds(0, len(group))], c_rs.at[which, at])
+            for q in group + ([me] if at == 0 else []):
+                cols = lane(q)
+                yield q, cols, skip[:, cols], c_recv[which, q].astype(F32)
+
+    for q, at, gain, value in returned(0):
+        mixed = value + gain * s2_send[q].astype(F32)
+        gq_o[:, at] = (bg[:, at].astype(F32) * mixed).astype(BF16)
+    arrived(g2_recv.at[pl.ds(0, n - 1)], g2_rs)
     for k in range(nc - 2, -1, -1):
         z = zorder[k]
-        send(g_send.at[:, band(z)], zg.at[mz], gz_ss.at[k], gz_rs.at[mz], {"chan": z})
-
-    transform(spec_f, me, rf[me])
-    for group in batches(peers):
-        for q in group:
-            arrived(rf.at[q], f_ss.at[q], f_rs.at[q], {"seq": q})
-        for q in group:
-            transform(spec_f, q, rf[q])
-    windowed(spec_f)
-    products(spec_s, False)
-    outputs(0, peers)
-    products(spec_u, True)
-    outputs(1, batches(peers)[0])
-
-    for q in peers:
-        arrived(s1.at[q], s1_ss.at[q], s1_rs.at[q], {"seq": q})
-    for q in range(n):
-        transform(spec_s, q, s1[q])
-    products(spec_s, False)
-    outputs(2, [])
-
-    for k in range(nc - 1):
-        z = zorder[k]
-        arrived(zg.at[z], gz_ss.at[k], gz_rs.at[z], {"chan": z})
-    for p in range(n):
-        acc = g_send[p, band(mz)].astype(F32)
-        for z in zorder:
-            acc += zg[z, p].astype(F32)
-        g2_send[p] = acc.astype(BF16)
-    for p in peers:
-        send(g2_send.at[p], g2_recv.at[me], g2_ss.at[p], g2_rs.at[me], {"seq": p})
-    g2_recv[me] = g2_send[me]
-    give_back(1, batches(peers)[1])
-    give_back(2, peers)
-
-    loaded(skip, fq)
-    for q in [me] + peers:
-        at = lane(q)
-        gain = skip[:, at]
-        if q is not me:
-            arrived(c_recv.at[0, q], c_ss.at[0, q], c_rs.at[0, q], {"seq": q})
-        mixed = c_recv[0, q].astype(F32) + gain * su_send[q, 0].astype(F32)
-        gq_o[:, at] = (bg[:, at].astype(F32) * mixed).astype(BF16)
-    for q in peers:
-        arrived(g2_recv.at[q], g2_ss.at[q], g2_rs.at[q], {"seq": q})
-    for k in range(nc - 2, -1, -1):
-        z = zorder[k]
-        send(g2_recv.at[pl.ds(z * per, per)], g3.at[mz], g3_ss.at[k], g3_rs.at[mz], {"chan": z})
+        send(g2_recv.at[pl.ds(z * per, per)], g3.at[mz], g3_ss, g3_rs, {"chan": z})
     for h in range(per):
         g3[mz, h] = g2_recv[mz * per + h]
-    for q in peers:
-        arrived(k_recv.at[q], k_ss.at[q], k_rs.at[q], {"seq": q})
+    arrived(k_recv.at[pl.ds(0, n - 1)], k_rs)
     for q in range(n):
         gs_o[:, q * w:(q + 1) * w] = k_recv[q, 0:1]
-    for q in [me] + peers:
-        at = lane(q)
-        gain = skip[:, at]
-        if q is not me:
-            arrived(c_recv.at[1, q], c_ss.at[1, q], c_rs.at[1, q], {"seq": q})
-        through = c_recv[1, q].astype(F32) + gain * su_send[q, 1].astype(F32)
+    for q, at, gain, value in returned(1):
+        through = value + gain * up_send[q].astype(F32)
         gk_o[:, at] = (through * bv[:, at].astype(F32)).astype(BF16)
         gv_o[:, at] = (through * bk[:, at].astype(F32)).astype(BF16)
-    for q in [me] + peers:
-        at = lane(q)
-        gain = skip[:, at]
-        if q is not me:
-            arrived(c_recv.at[2, q], c_ss.at[2, q], c_rs.at[2, q], {"seq": q})
-        mixed = c_recv[2, q].astype(F32) + gain * s1_send[q].astype(F32)
+    for q, at, gain, value in returned(2):
+        mixed = value + gain * s1_send[q].astype(F32)
         out_o[:, at] = (fq[:, at].astype(F32) * mixed).astype(BF16)
-    for k in range(nc - 1):
-        z = zorder[k]
-        arrived(g3.at[z], g3_ss.at[k], g3_rs.at[z], {"chan": z})
+    if nc > 1:
+        arrived(g3.at[pl.ds(0, nc - 1)], g3_rs)
     for z in range(nc):
         for h in range(per):
             gf_o[z * part:(z + 1) * part, h * w:(h + 1) * w] = g3[z, h].astype(F32)
 
-    for c in started:
-        c.wait_send()
-    for p in peers:
-        copy(fz.at[p], rf.at[me], f_ss.at[p], f_rs.at[me], {"seq": p}).wait_send()
-    for k in range(nc - 1):
-        for h in range(per):
-            chan_copy(k, h).wait_send()
+    sent(c_send.at[:, pl.ds(0, n - 1)], in_ss)
+    sent(c_send.at[:, pl.ds(0, n - 1)], c_ss)
+    sent(rf.at[pl.ds(0, n - 1)], f_ss)
+    sent(g2_send.at[pl.ds(0, n - 1)], g2_ss)
+    sent(k_recv.at[pl.ds(0, n - 1)], k_ss)
+    if nc > 1:
+        sent(fz.at[pl.ds(0, (nc - 1) * per)], z_ss)
+        sent(zg.at[pl.ds(0, nc - 1)], gz_ss)
+        sent(g3.at[pl.ds(0, nc - 1)], g3_ss)
 
 
 def store_all(*refs):
@@ -539,27 +552,25 @@
     per = filters.shape[1] // w
     part = rows // nc
     scale = 1.0 / math.sqrt(rows * n)
-    forward, inverse = (jnp.asarray(t, dtype=BF16) for t in block_tables(rows))
+    forward, inverse = (jnp.asarray(t, dtype=BF16) for t in block_tables(2 * rows))
     results = (
         *[pltpu.VMEM((rows, chan_width), BF16)] * 4, pltpu.VMEM(filters.shape, F32), pltpu.VMEM((1, chan_width), F32),
     )
     dma = pltpu.SemaphoreType.DMA
     block = (n, rows, w)
-    spectrum = (n, 2 * rows, w)
+    spectrum = (n // 2, 4 * rows, w)
     scratch = [
         *[pltpu.VMEM((rows, chan_width), BF16)] * 7, pltpu.VMEM(filters.shape, F32),
         pltpu.VMEM((1, chan_width), F32), pltpu.VMEM(forward.shape, BF16), pltpu.VMEM(inverse.shape, BF16),
         dma((11,)),
-        pltpu.VMEM((n, 2, rows, w), BF16), pltpu.VMEM(block, BF16), pltpu.VMEM(block, BF16),
-        pltpu.VMEM((n, 2, rows, w), BF16), pltpu.VMEM(block, BF16), pltpu.VMEM(block, BF16),
+        *[pltpu.VMEM(block, BF16)] * 8,
         *[pltpu.VMEM(spectrum, F32)] * 5,
         pltpu.VMEM((3,) + block, BF16), pltpu.VMEM((3,) + block, BF16),
         pltpu.VMEM(block, BF16), pltpu.VMEM((nc, n, part, w), BF16),
         pltpu.VMEM((n, part, w), BF16), pltpu.VMEM((n, part, w), BF16), pltpu.VMEM((nc, per, part, w), BF16),
         pltpu.VMEM((8, w), F32), pltpu.VMEM((n, 8, w), F32),
-        dma((n,)), dma((n,)), dma((n,)), dma((n,)), dma((n,)), dma((n,)),
-        dma((nc, per)), dma((nc, per)), pltpu.SemaphoreType.REGULAR, dma((3, n)), dma((3, n)),
-        dma((nc,)), dma((nc,)), dma((n,)), dma((n,)), dma((nc,)), dma((nc,)), dma((n,)), dma((n,)),
+        dma, *[dma((2,))] * 3, dma, dma((2,)), dma, dma((nc,)), pltpu.SemaphoreType.REGULAR,
+        dma, dma((3, 2)), *[dma] * 8,
     ]
     operands = (*args[:8], skip.reshape(1, chan_width), forward, inverse)
     hbm, vmem = (pl.BlockSpec(memory_space=m) for m in (pltpu.HBM, pltpu.VMEM))
@@ -589,7 +600,7 @@
     rows, chan_width = args[0].shape
     filter_width = args[7].shape[1]
     fits = chan_width % (n * LANES) == 0 and rows % (16 * nc) == 0 and rows % 32 == 0
-    fits = fits and n & (n - 1) == 0 and nc <= REACH + 2
+    fits = fits and n > 1 and n & (n - 1) == 0 and nc <= REACH + 2
     if fits and filter_width * nc == chan_width and filter_width % (chan_width // n) == 0:
         return fused_device(n, nc, *args)
     return per_device(*args)

time: 33.9 us -> 31.9 us (0.941)
  Pallas kernels: 33.1 us -> 31.1 us
    pallas_call x1, Pallas kernels: 32 us -> 30.1 us  [fused_device(): pl.pallas_call(functools.partial(kernel, n, nc, scale), out_shape=results...]
where the time goes in v4:
time: 31.9 us; the launch traced here: 31.8 us
  Pallas kernels  31.1 us (97%)
  between operations  0.64 us (2%)
    pallas_call x1, Pallas kernels, fused_device(): pl.pallas_call(functools.partial(kernel, n, nc, scale), out_shape=results...  30.1 us
    pallas_call x1, Pallas kernels, fused_device(): pl.pallas_call(store_all, out_shape=tuple((jax.ShapeDtypeStruct(o.shape,...  1.06 us

profile of v4, /device:TPU:0, one launch (start us, length us, event | category | flops | bytes accessed | tf_op | source)
XLA Modules:
  0.0 31.8 jit_solution(2629491220083949268)
XLA Ops:
  0.6 30.1 %shard_map.154 = (bf16[128,1024]{1,0:T(8,128)(2,1)S(1)}, bf16[128,1024]{1,0:T(8,128)(2,1)S(1)}, bf16[128,1024]{1,0:T(8,128)(2,1)S(1)}, bf16[128,1024]{1,0:T(8,12...) custom-call(bf16[128,1024]{1,0:T(8,128)(2,1)} %fq_h.1, bf16[128,1024]{1,0:T(8,128)(2,1)} %fk_h.1, ...), custom_call_target="tpu_custom_call" | custom-call | tf_op jit(solution)/shard_map/pallas_call | solution.py:577
  30.7 1.1 %shard_map.155 = (bf16[128,1024]{1,0:T(8,128)(2,1)}, bf16[128,1024]{1,0:T(8,128)(2,1)}, bf16[128,1024]{1,0:T(8,128)(2,1)}, bf16[128,1024]{1,0:T(8,128)(2,1)}, f32[128,256]{1,0:T(8,128)}, /*index=5*/f32[1,1024]{1,0:T(1,128)}) custom-call(bf16[128,1024]{1,0:T(8,128)(2,1)S(1)} %get-tuple-element.18.refs_0_, bf16[128,1024]{1,0:T(8,128)(2,1)S(1)} %get-tuple-element.19.refs_1_, ...), custom_call_target="tpu_custom_call" | custom-call | tf_op jit(solution)/shard_map/pallas_call | solution.py:587

commit v5 on v4

--- a/solution.py
+++ b/solution.py
@@ -213,15 +213,15 @@
     fq_h, fk_h, fv_h, bq_h, bk_h, bv_h, bg_h, filt_h, skip_h, fwd_h, inv_h,
     out_o, gq_o, gk_o, gv_o, gf_o, gs_o,
     fq, fk, fv, bq, bk, bv, bg, filt, skip, fwd_t, inv_t, in_sem,
-    s2_send, up_send, s1_send, fz, s2, up, s1, rf, spec_s, spec_u, spec_f, spec_w, prod,
-    c_send, c_recv, g_send, zg, g2_send, g2_recv, g3, k_send, k_recv,
+    s2_send, up_send, s1_send, f_send, fz, s2, up, s1, rf, spec_s, spec_u, spec_f, spec_w, spec_v, prod,
+    c_send, c_recv, g_send, zg, g2_send, g2_recv, k_send, k_recv,
     in_ss, s2_rs, up_rs, s1_rs, f_ss, f_rs, z_ss, z_rs, credit, c_ss, c_rs,
-    gz_ss, gz_rs, g2_ss, g2_rs, g3_ss, g3_rs, k_ss, k_rs,
+    gz_ss, gz_rs, g2_ss, g2_rs, k_ss, k_rs,
 ):
     rows, chan_width = fq.shape
     w = chan_width // n
     per = filt.shape[1] // w
-    part, half = rows // nc, rows // 2
+    part, unit = rows // nc, w // nc
     me = lax.axis_index("seq")
     mz = lax.axis_index("chan")
 
@@ -245,8 +245,18 @@
     def near(z):
         return (z - mz <= REACH) & (mz - z <= REACH)
 
-    def lane(p):
-        return pl.ds(pl.multiple_of(p * w, w), w)
+    slot = lax.broadcasted_iota(jnp.int32, (part, w), 1) // unit
+    own_slot = lax.rem(slot + nc - lax.rem(me, nc), nc)
+
+    def turned(x, k):
+        return pltpu.roll(x, (k % nc) * unit, 1) if k % nc else x
+
+    def pick(choices, shift=None):
+        out = choices[0]
+        for k in range(1, nc):
+            at = own_slot == k if shift is None else slot == (k + shift) % nc
+            out = jnp.where(at, choices[k], out)
+        return out
 
     def copy(src, dst, ss, rs, to):
         return pltpu.make_async_remote_copy(
@@ -298,28 +308,30 @@
         dst[c] = jnp.dot(fwd_t[...], block, preferred_element_type=F32)
 
     def gated(dst, left, right):
-        for p in range(n):
-            cols = slice(p * w, (p + 1) * w)
-            dst[p] = (left[:, cols].astype(F32) * right[:, cols].astype(F32)).astype(BF16)
+        for k in range(nc):
+            band_rows = slice(k * part, (k + 1) * part)
+            for hi in range(per):
+                pieces = []
+                for o in range(nc):
+                    cols = slice((o * per + hi) * w, (o * per + hi + 1) * w)
+                    value = left[band_rows, cols].astype(F32) * right[band_rows, cols].astype(F32)
+                    pieces.append(turned(value, o))
+                for j in range(nc):
+                    dst[hi * nc + j, band_rows] = pick(pieces, j).astype(BF16)
 
     loaded(bk, bv)
     gated(s2_send, bk, bv)
     loaded(filt)
-    for h in range(per):
-        fz[mz * per + h] = filt[:, h * w:(h + 1) * w].astype(BF16)
+    for hi in range(per):
+        cols = slice(hi * w, (hi + 1) * w)
+        pieces = [turned(filt[k * part:(k + 1) * part, cols], k) for k in range(nc)]
+        for j in range(nc):
+            f_send[hi * nc + j] = pick(pieces, j).astype(BF16)
     pl.semaphore_wait(barrier, greeted)
 
-    def forward(o, h):
-        p = o * per + h
-
-        @pl.when(p != me)
-        def _():
-            away = jnp.where(p // near_side == me // near_side, 0, 1) if near_side else 1
-            send(fz.at[p], rf.at[me], f_ss, f_rs.at[away], {"seq": p})
-
-    def chan_send(k):
-        block = fz.at[pl.ds(mz * per, per)]
-        send(block, block, z_ss, z_rs.at[mz], {"chan": zorder[k]})
+    for r, p in paired:
+        send(f_send.at[p], fz.at[mz, me], f_ss, f_rs.at[r // 2], {"seq": p})
+    fz[mz, me] = f_send[me]
 
     distant = ~near(zorder[-1]) if nc > 1 else None
     if nc > 1:
@@ -330,16 +342,6 @@
         @pl.when(vouch)
         def _():
             pl.semaphore_signal(credit, inc=1, device_id={"chan": o}, device_id_type=MESH)
-
-        @pl.when(~distant)
-        def _():
-            for k in range(nc - 2, -1, -1):
-                chan_send(k)
-
-        @pl.when(distant)
-        def _():
-            for k in range(nc - 3, -1, -1):
-                chan_send(k)
 
     def scatter(src, dst, ss, rs):
         for r, p in paired:
@@ -352,39 +354,32 @@
     scatter(up_send, up, in_ss, up_rs)
     loaded(fk, fv)
     gated(s1_send, fk, fv)
+
+    for i, c in enumerate(chips[::-1]):
+        fresh = fz.at[mz, pl.ds(2 * c, 2)]
+        arrived(fresh if i else fz.at[mz, pl.ds(0, 1)], f_rs.at[i])
+        if nc > 1 and i == 0:
+            @pl.when(distant)
+            def _():
+                pl.semaphore_wait(credit, 1)
+        for k in range(nc - 2, -1, -1):
+            send(fresh, fresh, z_ss, z_rs.at[mz], {"chan": zorder[k]})
     loaded(fwd_t, inv_t)
 
-    if nc > 1:
-        @pl.when(distant)
-        def _():
-            pl.semaphore_wait(credit, 1)
-            chan_send(nc - 2)
-
-    for k in range(nc - 1):
-        o = zorder[k]
-        arrived(fz.at[pl.ds(o * per, per)], z_rs.at[o])
-        for h in range(per):
-            if k == 0:
-                forward(mz, h)
-            forward(o, h)
-    for h in range(per if nc == 1 else 0):
-        forward(mz, h)
-    rf[me] = fz[me]
-
     sign = 1.0 - 2.0 * lax.rem(lax.broadcasted_iota(jnp.int32, (span, w), 0), 2).astype(F32)
 
-    def windowed(src):
-        spec_w[0] = src[0]
+    def windowed(dst, src):
+        dst[0] = src[0]
         for d in range(1, count):
-            spec_w[d, :span] = src[d, :span] - sign * src[d - 1, span:]
-            spec_w[d, span:] = src[d, span:] + sign * src[d - 1, :span]
-
-    def products(src, corr):
+            dst[d, :span] = src[d, :span] - sign * src[d - 1, span:]
+            dst[d, span:] = src[d, span:] + sign * src[d - 1, :span]
+
+    def products(win, src, corr):
         def tile(k, carry):
             re_at = pl.ds(pl.multiple_of(k * 16, 16), 16)
             im_at = pl.ds(pl.multiple_of(span + k * 16, 16), 16)
-            ar = [spec_w[d, re_at] for d in range(count)]
-            ai = [spec_w[d, im_at] for d in range(count)]
+            ar = [win[d, re_at] for d in range(count)]
+            ai = [win[d, im_at] for d in range(count)]
             xr = [src[d, re_at] for d in range(count)]
             xi = [src[d, im_at] for d in range(count)]
             for b in range(count):
@@ -428,31 +423,43 @@
                 give_back(which, [r for i in group for r in (n - 2 - 2 * i, n - 1 - 2 * i) if r])
         c_recv[which, me] = c_send[which, me]
 
-    def gather(bufs, rs, specs):
+    def gather(buf, sems, spec):
         for at, group in enumerate(batches(list(range(count))[::-1])):
-            for buf, sems in zip(bufs, rs):
-                if len(offsets[at]):
-                    arrived(buf.at[pl.ds(0, len(offsets[at]))], sems.at[at])
-            for buf, spec in zip(bufs, specs):
-                for i in group:
-                    transform(spec, chips[i], buf)
-
-    gather((s2, up), (s2_rs, up_rs), (spec_s, spec_u))
+            if len(offsets[at]):
+                arrived(buf.at[pl.ds(0, len(offsets[at]))], sems.at[at])
+            for i in group:
+                transform(spec, chips[i], buf)
+
+    gather(s2, s2_rs, spec_s)
     scatter(s1_send, s1, in_ss, s1_rs)
-    windowed(spec_s)
-    products(spec_u, True)
+    gather(up, up_rs, spec_u)
+    windowed(spec_v, spec_s)
+    products(spec_v, spec_u, True)
     for b in range(count):
-        halves(g_send, b, inverse(b) * scale)
-
-    def place(z):
-        return jnp.where(mz > z, mz - 1, mz)
-
-    def band(z):
-        return pl.ds(pl.multiple_of(z * part, part), part)
+        value = inverse(b) * scale
+        for h in range(2):
+            bands = [value[h * rows + k * part:h * rows + (k + 1) * part] for k in range(nc)]
+            for o in range(nc):
+                g_send[o, 2 * b + h] = pick([turned(bands[k], k - o) for k in range(nc)]).astype(BF16)
 
     for k in range(nc - 2, -1, -1):
         z = zorder[k]
-        send(g_send.at[:, band(z)], zg.at[place(z)], gz_ss, gz_rs, {"chan": z})
+        send(g_send.at[z], zg.at[jnp.where(mz > z, mz - 1, mz)], gz_ss, gz_rs, {"chan": z})
+
+    for z in zorder:
+        arrived(fz.at[z], z_rs.at[z])
+    for q in range(n):
+        pieces = [fz[o, q].astype(F32) for o in range(nc)]
+        for k in range(nc):
+            rf[q, k * part:(k + 1) * part] = pick([turned(pieces[o], o - k) for o in range(nc)]).astype(BF16)
+    for c in range(count):
+        transform(spec_f, c, rf)
+    windowed(spec_w, spec_f)
+    products(spec_w, spec_s, False)
+    outputs(0, True)
+
+    products(spec_w, spec_u, True)
+    outputs(1, True)
 
     total = jnp.zeros((1, w), F32)
     for q in range(n):
@@ -462,77 +469,72 @@
         send(k_send, k_recv.at[me], k_ss, k_rs, {"seq": p})
     k_recv[me] = k_send[...]
 
-    gather((rf,), (f_rs,), (spec_f,))
-    windowed(spec_f)
-    products(spec_s, False)
-    outputs(0, True)
-    products(spec_u, True)
-    outputs(1, False)
-    early, late = order[:n // 2], order[n // 2:]
-    give_back(1, early)
-
-    gather((s1,), (s1_rs,), (spec_s,))
-    products(spec_s, False)
-    outputs(2, False)
+    gather(s1, s1_rs, spec_s)
+    products(spec_w, spec_s, False)
+    outputs(2, True)
 
     if nc > 1:
         arrived(zg.at[pl.ds(0, nc - 1)], gz_rs)
     for p in range(n):
-        acc = g_send[p, band(mz)].astype(F32)
+        acc = g_send[mz, p].astype(F32)
         for k in range(nc - 1):
             acc += zg[k, p].astype(F32)
         g2_send[p] = acc.astype(BF16)
     for p in peers:
         send(g2_send.at[p], g2_recv.at[me], g2_ss, g2_rs, {"seq": p})
     g2_recv[me] = g2_send[me]
-    give_back(1, late)
-    give_back(2, order)
 
     loaded(skip, fq)
 
     def returned(which):
         for at in range(2):
-            group = [flipped(r) for r in offsets[at]]
-            if group:
-                arrived(c_recv.at[which, pl.ds(0, len(group))], c_rs.at[which, at])
-            for q in group + ([me] if at == 0 else []):
-                cols = lane(q)
-                yield q, cols, skip[:, cols], c_recv[which, q].astype(F32)
-
-    for q, at, gain, value in returned(0):
-        mixed = value + gain * s2_send[q].astype(F32)
-        gq_o[:, at] = (bg[:, at].astype(F32) * mixed).astype(BF16)
+            if len(offsets[at]):
+                arrived(c_recv.at[which, pl.ds(0, len(offsets[at]))], c_rs.at[which, at])
+        for k in range(nc):
+            at = slice(k * part, (k + 1) * part)
+            for hi in range(per):
+                values = [c_recv[which, hi * nc + j, at].astype(F32) for j in range(nc)]
+                for o in range(nc):
+                    cols = slice((o * per + hi) * w, (o * per + hi + 1) * w)
+                    yield (at, cols), skip[:, cols], turned(pick(values, o), -o)
+
+    def product(left, right, at):
+        return (left[at].astype(F32) * right[at].astype(F32)).astype(BF16).astype(F32)
+
+    for at, gain, value in returned(0):
+        mixed = value + gain * product(bk, bv, at)
+        gq_o[at] = (bg[at].astype(F32) * mixed).astype(BF16)
+    arrived(k_recv.at[pl.ds(0, n - 1)], k_rs)
+    sums = k_recv[...]
+    for hi in range(per):
+        for o in range(nc):
+            cols = slice((o * per + hi) * w, (o * per + hi + 1) * w)
+            value = sums[hi * nc]
+            for j in range(1, nc):
+                value = jnp.where(slot[:8] == (o + j) % nc, sums[hi * nc + j], value)
+            gs_o[:, cols] = turned(value, -o)[:1]
+    for at, gain, value in returned(1):
+        through = value + gain * product(bg, bq, at)
+        gk_o[at] = (through * bv[at].astype(F32)).astype(BF16)
+        gv_o[at] = (through * bk[at].astype(F32)).astype(BF16)
+    for at, gain, value in returned(2):
+        mixed = value + gain * product(fk, fv, at)
+        out_o[at] = (fq[at].astype(F32) * mixed).astype(BF16)
+
     arrived(g2_recv.at[pl.ds(0, n - 1)], g2_rs)
-    for k in range(nc - 2, -1, -1):
-        z = zorder[k]
-        send(g2_recv.at[pl.ds(z * per, per)], g3.at[mz], g3_ss, g3_rs, {"chan": z})
-    for h in range(per):
-        g3[mz, h] = g2_recv[mz * per + h]
-    arrived(k_recv.at[pl.ds(0, n - 1)], k_rs)
-    for q in range(n):
-        gs_o[:, q * w:(q + 1) * w] = k_recv[q, 0:1]
-    for q, at, gain, value in returned(1):
-        through = value + gain * up_send[q].astype(F32)
-        gk_o[:, at] = (through * bv[:, at].astype(F32)).astype(BF16)
-        gv_o[:, at] = (through * bk[:, at].astype(F32)).astype(BF16)
-    for q, at, gain, value in returned(2):
-        mixed = value + gain * s1_send[q].astype(F32)
-        out_o[:, at] = (fq[:, at].astype(F32) * mixed).astype(BF16)
-    if nc > 1:
-        arrived(g3.at[pl.ds(0, nc - 1)], g3_rs)
-    for z in range(nc):
-        for h in range(per):
-            gf_o[z * part:(z + 1) * part, h * w:(h + 1) * w] = g3[z, h].astype(F32)
+    for k in range(nc):
+        for hi in range(per):
+            value = pick([g2_recv[hi * nc + j].astype(F32) for j in range(nc)], k)
+            gf_o[k * part:(k + 1) * part, hi * w:(hi + 1) * w] = turned(value, -k)
 
     sent(c_send.at[:, pl.ds(0, n - 1)], in_ss)
     sent(c_send.at[:, pl.ds(0, n - 1)], c_ss)
-    sent(rf.at[pl.ds(0, n - 1)], f_ss)
+    sent(f_send.at[pl.ds(0, n - 1)], f_ss)
     sent(g2_send.at[pl.ds(0, n - 1)], g2_ss)
     sent(k_recv.at[pl.ds(0, n - 1)], k_ss)
     if nc > 1:
-        sent(fz.at[pl.ds(0, (nc - 1) * per)], z_ss)
+        sent(fz.at[pl.ds(0, nc - 1)], z_ss)
         sent(zg.at[pl.ds(0, nc - 1)], gz_ss)
-        sent(g3.at[pl.ds(0, nc - 1)], g3_ss)
 
 
 def store_all(*refs):
@@ -557,20 +559,20 @@
         *[pltpu.VMEM((rows, chan_width), BF16)] * 4, pltpu.VMEM(filters.shape, F32), pltpu.VMEM((1, chan_width), F32),
     )
     dma = pltpu.SemaphoreType.DMA
-    block = (n, rows, w)
+    block, bands = (n, rows, w), (n, part, w)
     spectrum = (n // 2, 4 * rows, w)
     scratch = [
         *[pltpu.VMEM((rows, chan_width), BF16)] * 7, pltpu.VMEM(filters.shape, F32),
         pltpu.VMEM((1, chan_width), F32), pltpu.VMEM(forward.shape, BF16), pltpu.VMEM(inverse.shape, BF16),
         dma((11,)),
-        *[pltpu.VMEM(block, BF16)] * 8,
-        *[pltpu.VMEM(spectrum, F32)] * 5,
+        *[pltpu.VMEM(block, BF16)] * 3, pltpu.VMEM(bands, BF16), pltpu.VMEM((nc,) + bands, BF16),
+        *[pltpu.VMEM(block, BF16)] * 4,
+        *[pltpu.VMEM(spectrum, F32)] * 6,
         pltpu.VMEM((3,) + block, BF16), pltpu.VMEM((3,) + block, BF16),
-        pltpu.VMEM(block, BF16), pltpu.VMEM((nc, n, part, w), BF16),
-        pltpu.VMEM((n, part, w), BF16), pltpu.VMEM((n, part, w), BF16), pltpu.VMEM((nc, per, part, w), BF16),
+        *[pltpu.VMEM((nc,) + bands, BF16)] * 2, *[pltpu.VMEM(bands, BF16)] * 2,
         pltpu.VMEM((8, w), F32), pltpu.VMEM((n, 8, w), F32),
-        dma, *[dma((2,))] * 3, dma, dma((2,)), dma, dma((nc,)), pltpu.SemaphoreType.REGULAR,
-        dma, dma((3, 2)), *[dma] * 8,
+        dma, *[dma((2,))] * 3, dma, dma((n // 2,)), dma, dma((nc,)), pltpu.SemaphoreType.REGULAR,
+        dma, dma((3, 2)), *[dma] * 6,
     ]
     operands = (*args[:8], skip.reshape(1, chan_width), forward, inverse)
     hbm, vmem = (pl.BlockSpec(memory_space=m) for m in (pltpu.HBM, pltpu.VMEM))
@@ -600,7 +602,7 @@
     rows, chan_width = args[0].shape
     filter_width = args[7].shape[1]
     fits = chan_width % (n * LANES) == 0 and rows % (16 * nc) == 0 and rows % 32 == 0
-    fits = fits and n > 1 and n & (n - 1) == 0 and nc <= REACH + 2
+    fits = fits and n % nc == 0 and n > 1 and n & (n - 1) == 0 and nc <= REACH + 2
     if fits and filter_width * nc == chan_width and filter_width % (chan_width // n) == 0:
         return fused_device(n, nc, *args)
     return per_device(*args)

time: 31.9 us -> 29.7 us (0.931)
  Pallas kernels: 31.1 us -> 28.9 us
    pallas_call x1, Pallas kernels: 30.1 us -> 27.8 us  [fused_device(): pl.pallas_call(functools.partial(kernel, n, nc, scale), out_shape=results...]
where the time goes in v5:
time: 29.7 us; the launch traced here: 29.5 us
  Pallas kernels  28.9 us (97%)
  between operations  0.64 us (2%)
    pallas_call x1, Pallas kernels, fused_device(): pl.pallas_call(functools.partial(kernel, n, nc, scale), out_shape=results...  27.8 us
    pallas_call x1, Pallas kernels, fused_device(): pl.pallas_call(store_all, out_shape=tuple((jax.ShapeDtypeStruct(o.shape,...  1.06 us

profile of v5, /device:TPU:0, one launch (start us, length us, event | category | flops | bytes accessed | tf_op | source)
XLA Modules:
  0.0 29.5 jit_solution(8867398643619891353)
XLA Ops:
  0.6 27.8 %shard_map.154 = (bf16[128,1024]{1,0:T(8,128)(2,1)S(1)}, bf16[128,1024]{1,0:T(8,128)(2,1)S(1)}, bf16[128,1024]{1,0:T(8,128)(2,1)S(1)}, bf16[128,1024]{1,0:T(8,12...) custom-call(bf16[128,1024]{1,0:T(8,128)(2,1)} %fq_h.1, bf16[128,1024]{1,0:T(8,128)(2,1)} %fk_h.1, ...), custom_call_target="tpu_custom_call" | custom-call | tf_op jit(solution)/shard_map/pallas_call | solution.py:579
  28.5 1.1 %shard_map.155 = (bf16[128,1024]{1,0:T(8,128)(2,1)}, bf16[128,1024]{1,0:T(8,128)(2,1)}, bf16[128,1024]{1,0:T(8,128)(2,1)}, bf16[128,1024]{1,0:T(8,128)(2,1)}, f32[128,256]{1,0:T(8,128)}, /*index=5*/f32[1,1024]{1,0:T(1,128)}) custom-call(bf16[128,1024]{1,0:T(8,128)(2,1)S(1)} %get-tuple-element.18.refs_0_, bf16[128,1024]{1,0:T(8,128)(2,1)S(1)} %get-tuple-element.19.refs_1_, ...), custom_call_target="tpu_custom_call" | custom-call | tf_op jit(solution)/shard_map/pallas_call | solution.py:589

commit v6 on v5

--- a/solution.py
+++ b/solution.py
@@ -213,7 +213,7 @@
     fq_h, fk_h, fv_h, bq_h, bk_h, bv_h, bg_h, filt_h, skip_h, fwd_h, inv_h,
     out_o, gq_o, gk_o, gv_o, gf_o, gs_o,
     fq, fk, fv, bq, bk, bv, bg, filt, skip, fwd_t, inv_t, in_sem,
-    s2_send, up_send, s1_send, f_send, fz, s2, up, s1, rf, spec_s, spec_u, spec_f, spec_w, spec_v, prod,
+    s2_send, up_send, s1_send, f_send, fz, s2, up, s1, rf, spec_s, spec_u, spec_f, spec_w, prod,
     c_send, c_recv, g_send, zg, g2_send, g2_recv, k_send, k_recv,
     in_ss, s2_rs, up_rs, s1_rs, f_ss, f_rs, z_ss, z_rs, credit, c_ss, c_rs,
     gz_ss, gz_rs, g2_ss, g2_rs, k_ss, k_rs,
@@ -273,22 +273,23 @@
         copy(buf, buf, ss, ss, {"seq": peers[0]}).wait_send()
 
     span, count = 2 * rows, n // 2
-    near_side = 2 * (count // 2)
+    parts = [list(range(count))[i:i + 2] for i in range(0, count, 2)]
 
     def side(r):
-        return 1 if r >= near_side else 0
-
-    offsets = (range(1, near_side), range(max(near_side, 1), n))
-
-    loads = {}
-    order_in = ((bk_h, bk), (bv_h, bv), (filt_h, filt), (bg_h, bg), (bq_h, bq), (fk_h, fk), (fv_h, fv))
-    for at, (far, dst) in enumerate(order_in + ((fwd_h, fwd_t), (inv_h, inv_t), (skip_h, skip), (fq_h, fq))):
-        loads[id(dst)] = pltpu.make_async_copy(far, dst, in_sem.at[at])
-        loads[id(dst)].start()
-
-    def loaded(*refs):
-        for ref in refs:
-            loads[id(ref)].wait()
+        return len(parts) - 1 - (count - 1 - r // 2) // 2
+
+    loads = (
+        ((bk_h, bk), (bv_h, bv)), ((filt_h, filt),), ((bg_h, bg), (bq_h, bq)), ((fk_h, fk), (fv_h, fv), (fq_h, fq)),
+        ((fwd_h, fwd_t),), ((inv_h, inv_t),), ((skip_h, skip),),
+    )
+    for at, group in enumerate(loads):
+        for far, dst in group:
+            pltpu.make_async_copy(far, dst, in_sem.at[at]).start()
+
+    def loaded(*which):
+        for at in which:
+            whole = loads[at][0][1] if len(loads[at]) == 1 else c_send.at[pl.ds(0, len(loads[at]))]
+            pltpu.make_async_copy(whole, whole, in_sem.at[at]).wait()
 
     barrier = pltpu.get_barrier_semaphore()
     for p in peers:
@@ -303,9 +304,11 @@
 
     chips = [flipped(r) // 2 for r in range(n - 2, 0, -2)] + [me // 2]
 
-    def transform(dst, c, src):
-        block = jnp.concatenate([src[2 * c], src[2 * c + 1]], axis=0)
-        dst[c] = jnp.dot(fwd_t[...], block, preferred_element_type=F32)
+    def transform(dst, group, src):
+        blocks = [jnp.concatenate([src[2 * c], src[2 * c + 1]], axis=0) for c in group]
+        value = jnp.dot(fwd_t[...], jnp.concatenate(blocks, axis=1), preferred_element_type=F32)
+        for i, c in enumerate(group):
+            dst[c] = value[:, i * w:(i + 1) * w]
 
     def gated(dst, left, right):
         for k in range(nc):
@@ -319,9 +322,9 @@
                 for j in range(nc):
                     dst[hi * nc + j, band_rows] = pick(pieces, j).astype(BF16)
 
-    loaded(bk, bv)
+    loaded(0)
     gated(s2_send, bk, bv)
-    loaded(filt)
+    loaded(1)
     for hi in range(per):
         cols = slice(hi * w, (hi + 1) * w)
         pieces = [turned(filt[k * part:(k + 1) * part, cols], k) for k in range(nc)]
@@ -349,10 +352,10 @@
         dst[me] = src[me]
 
     scatter(s2_send, s2, in_ss, s2_rs)
-    loaded(bg, bq)
+    loaded(2)
     gated(up_send, bg, bq)
     scatter(up_send, up, in_ss, up_rs)
-    loaded(fk, fv)
+    loaded(3)
     gated(s1_send, fk, fv)
 
     for i, c in enumerate(chips[::-1]):
@@ -363,23 +366,26 @@
             def _():
                 pl.semaphore_wait(credit, 1)
         for k in range(nc - 2, -1, -1):
-            send(fresh, fresh, z_ss, z_rs.at[mz], {"chan": zorder[k]})
-    loaded(fwd_t, inv_t)
-
-    sign = 1.0 - 2.0 * lax.rem(lax.broadcasted_iota(jnp.int32, (span, w), 0), 2).astype(F32)
-
-    def windowed(dst, src):
-        dst[0] = src[0]
-        for d in range(1, count):
-            dst[d, :span] = src[d, :span] - sign * src[d - 1, span:]
-            dst[d, span:] = src[d, span:] + sign * src[d - 1, :span]
-
-    def products(win, src, corr):
+            send(fresh, fresh, z_ss, z_rs, {"chan": zorder[k]})
+    loaded(4, 5)
+
+    sign = 1.0 - 2.0 * lax.rem(lax.broadcasted_iota(jnp.int32, (16, w), 0), 2).astype(F32)
+
+    def products(win, src, corr, raw=None):
         def tile(k, carry):
             re_at = pl.ds(pl.multiple_of(k * 16, 16), 16)
             im_at = pl.ds(pl.multiple_of(span + k * 16, 16), 16)
-            ar = [win[d, re_at] for d in range(count)]
-            ai = [win[d, im_at] for d in range(count)]
+            if raw is None:
+                ar = [win[d, re_at] for d in range(count)]
+                ai = [win[d, im_at] for d in range(count)]
+            else:
+                br = [raw[d, re_at] for d in range(count)]
+                bi = [raw[d, im_at] for d in range(count)]
+                ar = br[:1] + [br[d] - sign * bi[d - 1] for d in range(1, count)]
+                ai = bi[:1] + [bi[d] + sign * br[d - 1] for d in range(1, count)]
+                for d in range(count if win is not None else 0):
+                    win[d, re_at] = ar[d]
+                    win[d, im_at] = ai[d]
             xr = [src[d, re_at] for d in range(count)]
             xi = [src[d, im_at] for d in range(count)]
             for b in range(count):
@@ -394,68 +400,65 @@
                         ti = ar[d] * xi[c] + ai[d] * xr[c]
                     re = tr if re is None else re + tr
                     im = ti if im is None else im + ti
-                prod[b, re_at] = re
-                prod[b, im_at] = im
+                prod[b, re_at] = re.astype(BF16)
+                prod[b, im_at] = im.astype(BF16)
             return carry
 
         lax.fori_loop(0, span // 16, tile, 0)
 
-    def inverse(b):
-        return jnp.dot(inv_t[...], prod[b].astype(BF16), preferred_element_type=F32)
+    def inverse(group):
+        blocks = [prod[c] for c in group]
+        value = jnp.dot(inv_t[...], jnp.concatenate(blocks, axis=1), preferred_element_type=F32)
+        return [value[:, i * w:(i + 1) * w] for i in range(len(group))]
 
     def give_back(which, group):
         for r in group:
             p = flipped(r)
-            send(c_send.at[which, p], c_recv.at[which, me], c_ss, c_rs.at[which, side(r)], {"seq": p})
+            send(c_send.at[which, p], c_recv.at[which, me], c_ss, c_rs.at[which], {"seq": p})
 
     def halves(dst, c, value):
         dst[2 * c] = value[:rows].astype(BF16)
         dst[2 * c + 1] = value[rows:].astype(BF16)
 
-    def batches(items):
-        return [items[:len(items) // 2], items[len(items) // 2:]]
 
     def outputs(which, now):
-        for group in batches(list(range(count))):
-            for i in group:
-                halves(c_send.at[which], chips[i], inverse(chips[i]))
+        values = [inverse([chips[i] for i in group]) for group in parts]
+        for group, results in zip(parts, values):
+            for i, value in zip(group, results):
+                halves(c_send.at[which], chips[i], value)
             if now:
                 give_back(which, [r for i in group for r in (n - 2 - 2 * i, n - 1 - 2 * i) if r])
         c_recv[which, me] = c_send[which, me]
 
     def gather(buf, sems, spec):
-        for at, group in enumerate(batches(list(range(count))[::-1])):
-            if len(offsets[at]):
-                arrived(buf.at[pl.ds(0, len(offsets[at]))], sems.at[at])
-            for i in group:
-                transform(spec, chips[i], buf)
+        for at, group in enumerate(parts[::-1]):
+            arrived(buf.at[pl.ds(0, 2 * len(group) - (at == 0))], sems.at[at])
+            transform(spec, [chips[i] for i in group], buf)
 
     gather(s2, s2_rs, spec_s)
     scatter(s1_send, s1, in_ss, s1_rs)
     gather(up, up_rs, spec_u)
-    windowed(spec_v, spec_s)
-    products(spec_v, spec_u, True)
-    for b in range(count):
-        value = inverse(b) * scale
-        for h in range(2):
-            bands = [value[h * rows + k * part:h * rows + (k + 1) * part] for k in range(nc)]
-            for o in range(nc):
-                g_send[o, 2 * b + h] = pick([turned(bands[k], k - o) for k in range(nc)]).astype(BF16)
+    products(None, spec_u, True, spec_s)
+    for group in parts:
+        for b, value in zip(group, inverse(group)):
+            for h in range(2):
+                bands = [value[h * rows + k * part:h * rows + (k + 1) * part] * scale for k in range(nc)]
+                for o in range(nc):
+                    g_send[o, 2 * b + h] = pick([turned(bands[k], k - o) for k in range(nc)]).astype(BF16)
 
     for k in range(nc - 2, -1, -1):
         z = zorder[k]
         send(g_send.at[z], zg.at[jnp.where(mz > z, mz - 1, mz)], gz_ss, gz_rs, {"chan": z})
 
-    for z in zorder:
-        arrived(fz.at[z], z_rs.at[z])
+    if nc > 1:
+        arrived(fz.at[pl.ds(0, nc - 1)], z_rs)
     for q in range(n):
         pieces = [fz[o, q].astype(F32) for o in range(nc)]
         for k in range(nc):
             rf[q, k * part:(k + 1) * part] = pick([turned(pieces[o], o - k) for o in range(nc)]).astype(BF16)
-    for c in range(count):
-        transform(spec_f, c, rf)
-    windowed(spec_w, spec_f)
-    products(spec_w, spec_s, False)
+    for group in parts:
+        transform(spec_f, group, rf)
+    products(spec_w, spec_s, False, spec_f)
     outputs(0, True)
 
     products(spec_w, spec_u, True)
@@ -464,7 +467,7 @@
     total = jnp.zeros((1, w), F32)
     for q in range(n):
         total += jnp.sum(s2[q].astype(F32) * up[q].astype(F32), axis=0, keepdims=True)
-    k_send[...] = jnp.broadcast_to(total * scale, k_send.shape)
+    k_send[...] = total * scale
     for p in peers:
         send(k_send, k_recv.at[me], k_ss, k_rs, {"seq": p})
     k_recv[me] = k_send[...]
@@ -484,12 +487,10 @@
         send(g2_send.at[p], g2_recv.at[me], g2_ss, g2_rs, {"seq": p})
     g2_recv[me] = g2_send[me]
 
-    loaded(skip, fq)
+    loaded(6)
 
     def returned(which):
-        for at in range(2):
-            if len(offsets[at]):
-                arrived(c_recv.at[which, pl.ds(0, len(offsets[at]))], c_rs.at[which, at])
+        arrived(c_recv.at[which, pl.ds(0, n - 1)], c_rs.at[which])
         for k in range(nc):
             at = slice(k * part, (k + 1) * part)
             for hi in range(per):
@@ -511,8 +512,8 @@
             cols = slice((o * per + hi) * w, (o * per + hi + 1) * w)
             value = sums[hi * nc]
             for j in range(1, nc):
-                value = jnp.where(slot[:8] == (o + j) % nc, sums[hi * nc + j], value)
-            gs_o[:, cols] = turned(value, -o)[:1]
+                value = jnp.where(slot[:1] == (o + j) % nc, sums[hi * nc + j], value)
+            gs_o[:, cols] = turned(value, -o)
     for at, gain, value in returned(1):
         through = value + gain * product(bg, bq, at)
         gk_o[at] = (through * bv[at].astype(F32)).astype(BF16)
@@ -564,15 +565,15 @@
     scratch = [
         *[pltpu.VMEM((rows, chan_width), BF16)] * 7, pltpu.VMEM(filters.shape, F32),
         pltpu.VMEM((1, chan_width), F32), pltpu.VMEM(forward.shape, BF16), pltpu.VMEM(inverse.shape, BF16),
-        dma((11,)),
+        dma((7,)),
         *[pltpu.VMEM(block, BF16)] * 3, pltpu.VMEM(bands, BF16), pltpu.VMEM((nc,) + bands, BF16),
         *[pltpu.VMEM(block, BF16)] * 4,
-        *[pltpu.VMEM(spectrum, F32)] * 6,
+        *[pltpu.VMEM(spectrum, F32)] * 4, pltpu.VMEM(spectrum, BF16),
         pltpu.VMEM((3,) + block, BF16), pltpu.VMEM((3,) + block, BF16),
         *[pltpu.VMEM((nc,) + bands, BF16)] * 2, *[pltpu.VMEM(bands, BF16)] * 2,
-        pltpu.VMEM((8, w), F32), pltpu.VMEM((n, 8, w), F32),
-        dma, *[dma((2,))] * 3, dma, dma((n // 2,)), dma, dma((nc,)), pltpu.SemaphoreType.REGULAR,
-        dma, dma((3, 2)), *[dma] * 6,
+        pltpu.VMEM((1, w), F32), pltpu.VMEM((n, 1, w), F32),
+        dma, *[dma(((n + 2) // 4,))] * 3, dma, dma((n // 2,)), dma, dma, pltpu.SemaphoreType.REGULAR,
+        dma, dma((3,)), *[dma] * 6,
     ]
     operands = (*args[:8], skip.reshape(1, chan_width), forward, inverse)
     hbm, vmem = (pl.BlockSpec(memory_space=m) for m in (pltpu.HBM, pltpu.VMEM))

time: 29.7 us -> 29.3 us (0.987)
  Pallas kernels: 28.9 us -> 28.5 us
    pallas_call x1, Pallas kernels: 27.8 us -> 27.4 us  [fused_device(): pl.pallas_call(functools.partial(kernel, n, nc, scale), out_shape=results...]
where the time goes in v6:
time: 29.3 us; the launch traced here: 29.1 us
  Pallas kernels  28.5 us (97%)
  between operations  0.64 us (2%)
    pallas_call x1, Pallas kernels, fused_device(): pl.pallas_call(functools.partial(kernel, n, nc, scale), out_shape=results...  27.4 us
    pallas_call x1, Pallas kernels, fused_device(): pl.pallas_call(store_all, out_shape=tuple((jax.ShapeDtypeStruct(o.shape,...  1.06 us

profile of v6, /device:TPU:0, one launch (start us, length us, event | category | flops | bytes accessed | tf_op | source)
XLA Modules:
  0.0 29.1 jit_solution(3383907475910584049)
XLA Ops:
  0.6 27.4 %shard_map.154 = (bf16[128,1024]{1,0:T(8,128)(2,1)S(1)}, bf16[128,1024]{1,0:T(8,128)(2,1)S(1)}, bf16[128,1024]{1,0:T(8,128)(2,1)S(1)}, bf16[128,1024]{1,0:T(8,12...) custom-call(bf16[128,1024]{1,0:T(8,128)(2,1)} %fq_h.1, bf16[128,1024]{1,0:T(8,128)(2,1)} %fk_h.1, ...), custom_call_target="tpu_custom_call" | custom-call | tf_op jit(solution)/shard_map/pallas_call | solution.py:580
  28.1 1.1 %shard_map.155 = (bf16[128,1024]{1,0:T(8,128)(2,1)}, bf16[128,1024]{1,0:T(8,128)(2,1)}, bf16[128,1024]{1,0:T(8,128)(2,1)}, bf16[128,1024]{1,0:T(8,128)(2,1)}, f32[128,256]{1,0:T(8,128)}, /*index=5*/f32[1,1024]{1,0:T(1,128)}) custom-call(bf16[128,1024]{1,0:T(8,128)(2,1)S(1)} %get-tuple-element.18.refs_0_, bf16[128,1024]{1,0:T(8,128)(2,1)S(1)} %get-tuple-element.19.refs_1_, ...), custom_call_target="tpu_custom_call" | custom-call | tf_op jit(solution)/shard_map/pallas_call | solution.py:590

commit v7 on v6

--- a/solution.py
+++ b/solution.py
@@ -442,9 +442,9 @@
     for group in parts:
         for b, value in zip(group, inverse(group)):
             for h in range(2):
-                bands = [value[h * rows + k * part:h * rows + (k + 1) * part] * scale for k in range(nc)]
+                bands = [(value[h * rows + k * part:h * rows + (k + 1) * part] * scale).astype(BF16) for k in range(nc)]
                 for o in range(nc):
-                    g_send[o, 2 * b + h] = pick([turned(bands[k], k - o) for k in range(nc)]).astype(BF16)
+                    g_send[o, 2 * b + h] = pick([turned(bands[k], k - o) for k in range(nc)])
 
     for k in range(nc - 2, -1, -1):
         z = zorder[k]
@@ -453,9 +453,9 @@
     if nc > 1:
         arrived(fz.at[pl.ds(0, nc - 1)], z_rs)
     for q in range(n):
-        pieces = [fz[o, q].astype(F32) for o in range(nc)]
+        pieces = [fz[o, q] for o in range(nc)]
         for k in range(nc):
-            rf[q, k * part:(k + 1) * part] = pick([turned(pieces[o], o - k) for o in range(nc)]).astype(BF16)
+            rf[q, k * part:(k + 1) * part] = pick([turned(pieces[o], o - k) for o in range(nc)])
     for group in parts:
         transform(spec_f, group, rf)
     products(spec_w, spec_s, False, spec_f)

time: 29.3 us -> 29.3 us (level)
  no operation moved by 1% of the time
where the time goes in v7:
time: 29.3 us; the launch traced here: 29.1 us
  Pallas kernels  28.5 us (97%)
  between operations  0.64 us (2%)
    pallas_call x1, Pallas kernels, fused_device(): pl.pallas_call(functools.partial(kernel, n, nc, scale), out_shape=results...  27.4 us
    pallas_call x1, Pallas kernels, fused_device(): pl.pallas_call(store_all, out_shape=tuple((jax.ShapeDtypeStruct(o.shape,...  1.06 us

profile of v7, /device:TPU:0, one launch (start us, length us, event | category | flops | bytes accessed | tf_op | source)
XLA Modules:
  0.0 29.1 jit_solution(16656777023385160381)
XLA Ops:
  0.6 27.4 %shard_map.154 = (bf16[128,1024]{1,0:T(8,128)(2,1)S(1)}, bf16[128,1024]{1,0:T(8,128)(2,1)S(1)}, bf16[128,1024]{1,0:T(8,128)(2,1)S(1)}, bf16[128,1024]{1,0:T(8,12...) custom-call(bf16[128,1024]{1,0:T(8,128)(2,1)} %fq_h.1, bf16[128,1024]{1,0:T(8,128)(2,1)} %fk_h.1, ...), custom_call_target="tpu_custom_call" | custom-call | tf_op jit(solution)/shard_map/pallas_call | solution.py:580
  28.1 1.1 %shard_map.155 = (bf16[128,1024]{1,0:T(8,128)(2,1)}, bf16[128,1024]{1,0:T(8,128)(2,1)}, bf16[128,1024]{1,0:T(8,128)(2,1)}, bf16[128,1024]{1,0:T(8,128)(2,1)}, f32[128,256]{1,0:T(8,128)}, /*index=5*/f32[1,1024]{1,0:T(1,128)}) custom-call(bf16[128,1024]{1,0:T(8,128)(2,1)S(1)} %get-tuple-element.18.refs_0_, bf16[128,1024]{1,0:T(8,128)(2,1)S(1)} %get-tuple-element.19.refs_1_, ...), custom_call_target="tpu_custom_call" | custom-call | tf_op jit(solution)/shard_map/pallas_call | solution.py:590
